TPU v7x, 32 devices: a whole 2x2x4 slice. The times are simulated.
32 devices in a mesh: row: 8 (over y, x, core), col: 4 (over z).
Axes of the slice: x: 2, y: 2, z: 4, core: 2. Of those that a mesh axis runs over, the one named last changes fastest.
Arguments:
- tensor: float32 [128, 128, 768], P('row', 'col'), may hold values from -6 to 6
- start_one: float32 [128, 64], P('row'), may hold values from -0.5 to 0.5
- start_two: float32 [128, 64], P('col'), may hold values from -0.5 to 0.5
- start_three: float32 [768, 64], replicated, may hold values from -0.21875 to 0.21875
Outputs:
- factor_one: float32 [128, 64], replicated
- factor_two: float32 [128, 64], replicated
- factor_three: float32 [768, 64], replicated
- core: float32 [64, 64, 64], P(None, 'row', 'col')
All inputs are finite; a program needn't handle non-finite values.
Results may differ from a plain program's by a relative error of at most 0.0003.
Values sent between devices are 32-bit elements; how exact they have to be, the bound alone decides.
A program may use at most 64 MiB of HBM per device.

v0:
```python
import functools
import math

import jax
import jax.numpy as jnp
from jax import lax
from jax.experimental import pallas as pl
from jax.experimental.pallas import tpu as pltpu
from jax.sharding import PartitionSpec as P

STEPS = 4


HIGHEST = lax.Precision.HIGHEST
MESH = pl.DeviceIdType.MESH
SUBLANES = 8
LANES = 128


def product(left, right):
    return jnp.dot(left, right, precision=HIGHEST, preferred_element_type=jnp.float32)


def left_product(left, right):
    return lax.dot_general(
        left, right, (((0,), (0,)), ((), ())), precision=HIGHEST, preferred_element_type=jnp.float32
    )


def right_product(left, right):
    return lax.dot_general(
        left, right, (((1,), (1,)), ((), ())), precision=HIGHEST, preferred_element_type=jnp.float32
    )


def cross_product(left, right):
    return lax.dot_general(
        left, right, (((0,), (1,)), ((), ())), precision=HIGHEST, preferred_element_type=jnp.float32
    )


def orthonormal(matrix, inner):
    lower = jnp.linalg.cholesky(inner)
    return jax.scipy.linalg.solve_triangular(lower, matrix.T, lower=True).T


def settle(gram_whole, basis):
    for iteration in range(STEPS):
        image = product(gram_whole, basis)
        basis = orthonormal(image, left_product(image, image))
    return basis


def general(tensor, start_one, start_two, start_three):
    rows_one, rows_two, depth = tensor.shape
    rank = start_three.shape[1]
    flat = tensor.reshape(rows_one * rows_two, depth)
    contracted = cross_product(start_three, flat).reshape(rank, rows_one, rows_two)
    part_one = jnp.einsum("cij,jb->ibc", contracted, start_two, precision=HIGHEST).reshape(
        rows_one, rank * rank
    )
    slab_one = lax.psum_scatter(part_one, "col", scatter_dimension=1, tiled=True)
    slab_rows_one = lax.all_gather(slab_one, "row", axis=0, tiled=True)
    gram_one = lax.psum(right_product(slab_rows_one, slab_rows_one), "col")
    basis_one = settle(gram_one, lax.all_gather(start_one, "row", axis=0, tiled=True))
    own_one = lax.dynamic_slice_in_dim(basis_one, lax.axis_index("row") * rows_one, rows_one, 0)
    part_two = jnp.einsum("cij,ia->jac", contracted, own_one, precision=HIGHEST).reshape(
        rows_two, rank * rank
    )
    slab_two = lax.psum_scatter(part_two, "row", scatter_dimension=1, tiled=True)
    slab_rows_two = lax.all_gather(slab_two, "col", axis=0, tiled=True)
    gram_two = lax.psum(right_product(slab_rows_two, slab_rows_two), "row")
    basis_two = settle(gram_two, lax.all_gather(start_two, "col", axis=0, tiled=True))
    own_two = lax.dynamic_slice_in_dim(basis_two, lax.axis_index("col") * rows_two, rows_two, 0)
    received = lax.all_to_all(tensor, "row", split_axis=2, concat_axis=0, tiled=True)
    count, items, cells = received.shape
    merged = left_product(basis_one, received.reshape(count, items * cells))
    mixed = merged.reshape(rank, items, cells)
    part_three = jnp.einsum("ajk,jb->kba", mixed, own_two, precision=HIGHEST)
    cells_here = part_three.shape[0]
    slab_three = lax.psum_scatter(
        part_three.reshape(cells_here, rank * rank), "col", scatter_dimension=1, tiled=True
    )
    gram_part_three = right_product(slab_three, lax.all_gather(slab_three, "row", axis=0, tiled=True))
    gram_three = lax.psum(gram_part_three, "col")
    basis_three = start_three
    own_three = start_three
    for iteration in range(STEPS):
        image = product(gram_three, basis_three)
        inner = lax.psum(left_product(image, image), "row")
        own_three = orthonormal(image, inner)
        basis_three = lax.all_gather(own_three, "row", axis=0, tiled=True)
    core_part = left_product(own_three, slab_three)
    core_part = core_part.reshape(rank, core_part.shape[1] // rank, rank)
    core = lax.psum_scatter(core_part, "row", scatter_dimension=2, tiled=True).transpose(0, 2, 1)
    factor_one = basis_one * math.sqrt(basis_one.shape[0])
    factor_two = basis_two * math.sqrt(basis_two.shape[0])
    factor_three = basis_three * math.sqrt(basis_three.shape[0])
    return (factor_one, factor_two, factor_three, core)


def inverse_factor(inner):
    n = inner.shape[0]
    groups = n // SUBLANES
    eye = (
        lax.broadcasted_iota(jnp.int32, (n, n), 0) == lax.broadcasted_iota(jnp.int32, (n, n), 1)
    ).astype(jnp.float32)
    whole = jnp.concatenate([inner, eye], axis=1)
    width = whole.shape[1]
    rows = [whole[g * SUBLANES : (g + 1) * SUBLANES] for g in range(groups)]
    sub = lax.broadcasted_iota(jnp.int32, (SUBLANES, width), 0)
    pivots = [None] * n
    shape = (SUBLANES, width)
    for base in range(groups):
        columns = [
            [jnp.broadcast_to(rows[g][:, k : k + 1], shape) for g in range(base, groups)]
            for k in range(base * SUBLANES, (base + 1) * SUBLANES)
        ]
        for t in range(SUBLANES):
            pivot = jnp.broadcast_to(columns[t][0][t : t + 1, :], shape)
            scale = 1.0 / pivot
            pivots[base * SUBLANES + t] = pivot
            row = jnp.broadcast_to(rows[base][t : t + 1, :], shape)
            heads = [
                jnp.broadcast_to(columns[s][0][t : t + 1, :], shape) for s in range(t + 1, SUBLANES)
            ]
            for g in range(base, groups):
                factor = columns[t][g - base] * scale
                if g == base:
                    factor = jnp.where(sub > t, factor, 0.0)
                rows[g] = rows[g] - factor * row
                for s in range(t + 1, SUBLANES):
                    columns[s][g - base] = columns[s][g - base] - factor * heads[s - t - 1]
    out = []
    for g in range(groups):
        held = pivots[g * SUBLANES]
        for t in range(1, SUBLANES):
            held = jnp.where(sub == t, pivots[g * SUBLANES + t], held)
        out.append(rows[g] * lax.rsqrt(held))
    return jnp.concatenate(out, axis=0)[:, n:]


def orth(image):
    return right_product(image, inverse_factor(left_product(image, image)))


def steps_on(gram_ref, start_ref, basis_ref):
    basis_ref[...] = start_ref[...]

    def one(_, carry):
        basis_ref[...] = orth(product(gram_ref[...], basis_ref[...]))
        return carry

    lax.fori_loop(0, STEPS, one, 0)


def gram_one_kernel(held_ref, start_ref, gram_ref):
    slabs = [product(held_ref[c], start_ref[...]) for c in range(held_ref.shape[0])]
    total = right_product(slabs[0], slabs[0])
    for slab in slabs[1:]:
        total = total + right_product(slab, slab)
    gram_ref[...] = total


def mode_one_kernel(gram_ref, start_ref, held_ref, basis_ref, factor_ref, next_ref):
    steps_on(gram_ref, start_ref, basis_ref)
    basis = basis_ref[...]
    factor_ref[...] = (basis * math.sqrt(basis.shape[0])).T
    total = None
    for c in range(held_ref.shape[0]):
        slab = left_product(held_ref[c], basis)
        term = right_product(slab, slab)
        total = term if total is None else total + term
    next_ref[...] = total


def lane_groups(width):
    return lax.div(lax.broadcasted_iota(jnp.int32, (1, LANES), 1), width)


def shifted(value, amount):
    amount = amount % LANES
    return value if amount == 0 else pltpu.roll(value, amount, 1)


def mode_two_kernel(n_row, n_col, gram_ref, start_ref, one_ref, cube_ref, factor_ref, send_ref, basis_ref, cube, mixed):
    n, cells, span = cube_ref.shape
    width = LANES // n_col
    rows_one = span // width
    group = lane_groups(width)
    for row in range(n_row):
        for tile in range(span // LANES):
            blocks = [cube_ref[row * n_col + q, :, tile * LANES : (tile + 1) * LANES] for q in range(n_col)]
            for s in range(n_col):
                held = blocks[0]
                held = shifted(held, -s * width)
                for q in range(1, n_col):
                    held = jnp.where(group == q, shifted(blocks[q], (q - s) * width), held)
                item = row * rows_one + tile * n_col + s
                cube[item * cells : (item + 1) * cells, :] = held
    count, rank = one_ref.shape
    one = one_ref[...]
    for k in range(cells):
        face = cube[pl.ds(k, count, stride=cells), :]
        mixed[k * rank : (k + 1) * rank, :] = left_product(one, face)
    steps_on(gram_ref, start_ref, basis_ref)
    basis = basis_ref[...]
    factor_ref[...] = (basis * math.sqrt(basis.shape[0])).T
    wide = jnp.concatenate([basis, jnp.zeros((basis.shape[0], LANES - rank), jnp.float32)], axis=1)
    own_a, own_b = rank // n_row, rank // n_col
    group = lane_groups(own_b)
    for row in range(n_row):
        rows = [mixed[pl.ds(row * own_a + s, cells, stride=rank), :] for s in range(own_a)]
        slabs = product(jnp.concatenate(rows, axis=0), wide)
        for q in range(n_col):
            held = None
            for s in range(own_a):
                moved = shifted(slabs[s * cells : (s + 1) * cells], (s - q) * own_b)
                held = moved if held is None else jnp.where(group == s, moved, held)
            send_ref[row * n_col + q] = held


def pack(image):
    half = image.shape[0] // 2
    return jnp.concatenate([image[:half], image[half:]], axis=1)


def unpack(packed):
    half = packed.shape[1] // 2
    return jnp.concatenate([packed[:, :half], packed[:, half:]], axis=0)


def on_core(kernel, shapes, *operands, scratch=()):
    outs = [jax.ShapeDtypeStruct(shape, jnp.float32) for shape in shapes]
    spec = pl.BlockSpec(memory_space=pltpu.VMEM)
    cost = pl.CostEstimate(flops=2 * 10**9, bytes_accessed=2 * 10**6, transcendentals=0)
    return pl.pallas_call(
        kernel,
        out_shape=outs,
        in_specs=[spec] * len(operands),
        out_specs=[spec] * len(outs),
        scratch_shapes=[pltpu.VMEM(shape, jnp.float32) for shape in scratch],
        cost_estimate=cost,
    )(*operands)


def row_peer(n_row, d):
    return (lax.rem(lax.axis_index("row") + d, n_row), lax.axis_index("col"))


def col_peer(n_col, d):
    return (lax.axis_index("row"), lax.rem(lax.axis_index("col") + d, n_col))


def sum_body(n_row, n_col, x_ref, o_ref, parts, planes, s1, r1, s2, r2, s3, r3):
    row, col = lax.axis_index("row"), lax.axis_index("col")
    count = x_ref.shape[0] // n_row

    def mine(which):
        return pl.ds(pl.multiple_of(which * count, SUBLANES), count)

    def copies(n, peer, source, target, send, recv):
        made = [
            pltpu.make_async_remote_copy(
                src_ref=source(d),
                dst_ref=target(d),
                send_sem=send.at[d],
                recv_sem=recv.at[d],
                device_id=peer(n, d),
                device_id_type=MESH,
            )
            for d in range(1, n)
        ]
        for copy in made:
            copy.start()
        return made

    first = copies(
        n_row, row_peer, lambda d: x_ref.at[mine(row_peer(n_row, d)[0])], lambda d: parts.at[d], s1, r1
    )
    total = x_ref[mine(row), :]
    for d in range(1, n_row):
        first[d - 1].wait_recv()
        total = total + parts[d]
    planes[col] = total
    second = copies(n_col, col_peer, lambda d: planes.at[col], lambda d: planes.at[col], s2, r2)
    for copy in second:
        copy.wait_recv()
    total = planes[0]
    for q in range(1, n_col):
        total = total + planes[q]
    o_ref[mine(row), :] = total
    third = copies(n_row, row_peer, lambda d: o_ref.at[mine(row)], lambda d: o_ref.at[mine(row)], s3, r3)
    for copy in third:
        copy.wait_recv()
    for copy in first + second + third:
        copy.wait_send()


def sum_kernel(n_row, n_col, *refs):
    barrier = pltpu.get_barrier_semaphore()
    for d in range(1, n_row):
        pl.semaphore_signal(barrier, inc=1, device_id=row_peer(n_row, d), device_id_type=MESH)
    for d in range(1, n_col):
        pl.semaphore_signal(barrier, inc=1, device_id=col_peer(n_col, d), device_id_type=MESH)
    pl.semaphore_wait(barrier, n_row + n_col - 2)
    sum_body(n_row, n_col, *refs)


def sum_all(n_row, n_col, name, collective_id, x):
    spec = pl.BlockSpec(memory_space=pltpu.VMEM)
    count = x.shape[0] // n_row
    dma = pltpu.SemaphoreType.DMA
    return pl.pallas_call(
        functools.partial(sum_kernel, n_row, n_col),
        out_shape=jax.ShapeDtypeStruct(x.shape, x.dtype),
        in_specs=[spec],
        out_specs=spec,
        scratch_shapes=[
            pltpu.VMEM((n_row, count, x.shape[1]), x.dtype),
            pltpu.VMEM((n_col, count, x.shape[1]), x.dtype),
            dma((n_row,)),
            dma((n_row,)),
            dma((n_col,)),
            dma((n_col,)),
            dma((n_row,)),
            dma((n_row,)),
        ],
        compiler_params=pltpu.CompilerParams(collective_id=collective_id, has_side_effects=True),
        cost_estimate=pl.CostEstimate(flops=10**9, bytes_accessed=10**7, transcendentals=0),
        name=name,
    )(x)


def place(n_row, n_col):
    return lax.axis_index("row") * n_col + lax.axis_index("col")


def greet_all(n_row, n_col):
    n = n_row * n_col
    me = place(n_row, n_col)
    barrier = pltpu.get_barrier_semaphore()

    def one(d, carry):
        peer = lax.rem(me + d, n)
        pl.semaphore_signal(
            barrier, inc=1, device_id=(peer // n_col, lax.rem(peer, n_col)), device_id_type=MESH
        )
        return carry

    lax.fori_loop(1, n, one, 0)
    pl.semaphore_wait(barrier, n - 1)


def exchange_copy(n_row, n_col, d, source, target, send, recv):
    n = n_row * n_col
    me = place(n_row, n_col)
    peer = lax.rem(me + d, n)
    return pltpu.make_async_remote_copy(
        src_ref=source.at[peer],
        dst_ref=target.at[me],
        send_sem=send.at[d],
        recv_sem=recv.at[d],
        device_id=(peer // n_col, lax.rem(peer, n_col)),
        device_id_type=MESH,
    )


def start_exchange(n_row, n_col, *refs):
    def one(d, carry):
        exchange_copy(n_row, n_col, d, *refs).start()
        return carry

    lax.fori_loop(1, n_row * n_col, one, 0)


def end_exchange(n_row, n_col, *refs):
    def one(d, carry):
        exchange_copy(n_row, n_col, d, *refs).wait()
        return carry

    lax.fori_loop(1, n_row * n_col, one, 0)


def front_kernel(
    n_row, n_col, flat_ref, three_ref, one_ref, two_ref,
    held_ref, turned_ref, all_one_ref, all_two_ref,
    parted, send, recv, s1, r1, s2, r2,
):
    row, col = lax.axis_index("row"), lax.axis_index("col")
    me = place(n_row, n_col)
    n, share, span = parted.shape
    contracted = right_product(three_ref[...], flat_ref[...])
    for d in range(n):
        parted[d] = contracted[d * share : (d + 1) * share]
    greet_all(n_row, n_col)
    start_exchange(n_row, n_col, parted, held_ref, send, recv)
    count_one, count_two = one_ref.shape[0], two_ref.shape[0]
    own_one = pl.ds(pl.multiple_of(row * count_one, SUBLANES), count_one)
    own_two = pl.ds(pl.multiple_of(col * count_two, SUBLANES), count_two)
    made = []
    for d in range(1, n_row):
        made.append(
            pltpu.make_async_remote_copy(
                src_ref=one_ref,
                dst_ref=all_one_ref.at[own_one],
                send_sem=s1.at[d],
                recv_sem=r1.at[d],
                device_id=(lax.rem(row + d, n_row), col),
                device_id_type=MESH,
            )
        )
    for d in range(1, n_col):
        made.append(
            pltpu.make_async_remote_copy(
                src_ref=two_ref,
                dst_ref=all_two_ref.at[own_two],
                send_sem=s2.at[d],
                recv_sem=r2.at[d],
                device_id=(row, lax.rem(col + d, n_col)),
                device_id_type=MESH,
            )
        )
    for copy in made:
        copy.start()
    held_ref[me] = parted[me]
    all_one_ref[own_one, :] = one_ref[...]
    all_two_ref[own_two, :] = two_ref[...]
    turned_ref[...] = flat_ref[...].T
    for copy in made:
        copy.wait()
    end_exchange(n_row, n_col, parted, held_ref, send, recv)


def tail_kernel(
    n_row, n_col, send_ref, start_ref, factor_ref, core_ref,
    slab_ref, image, summed, parts, planes, send, recv, s1, r1, s2, r2, s3, r3,
):
    me = place(n_row, n_col)
    greet_all(n_row, n_col)
    start_exchange(n_row, n_col, send_ref, slab_ref, send, recv)
    slab_ref[me] = send_ref[me]
    end_exchange(n_row, n_col, send_ref, slab_ref, send, recv)
    n, cells, width = slab_ref.shape

    def slab():
        return slab_ref[...].reshape(n * cells, width)

    image[...] = pack(product(slab(), cross_product(slab(), start_ref[...])))

    def one(step, carry):
        turn = lax.rem(step, 2)
        sum_body(
            n_row, n_col, image, summed, parts, planes.at[turn],
            s1, r1, s2.at[turn], r2.at[turn], s3, r3,
        )
        now = unpack(summed[...])
        inverse = inverse_factor(left_product(now, now))

        @pl.when(step < STEPS - 1)
        def _():
            basis = right_product(now, inverse)
            image[...] = pack(product(slab(), left_product(slab(), basis)))

        @pl.when(step == STEPS - 1)
        def _():
            turned = right_product(inverse, now)
            factor_ref[...] = turned * math.sqrt(turned.shape[1])
            core_ref[...] = cross_product(slab(), turned)

        return carry

    lax.fori_loop(0, STEPS, one, 0)


def linked(kernel, n_row, n_col, collective_id, shapes, scratch, *operands):
    outs = [jax.ShapeDtypeStruct(shape, jnp.float32) for shape in shapes]
    spec = pl.BlockSpec(memory_space=pltpu.VMEM)
    return pl.pallas_call(
        functools.partial(kernel, n_row, n_col),
        out_shape=outs,
        in_specs=[spec] * len(operands),
        out_specs=[spec] * len(outs),
        scratch_shapes=scratch,
        compiler_params=pltpu.CompilerParams(collective_id=collective_id, has_side_effects=True),
        cost_estimate=pl.CostEstimate(flops=10**9, bytes_accessed=10**7, transcendentals=0),
    )(*operands)


def shared(n_row, n_col, tensor, start_one, start_two, start_three):
    rows_one, rows_two, depth = tensor.shape
    rank = start_three.shape[1]
    both = ("row", "col")
    n = n_row * n_col
    n_one, n_two = rows_one * n_row, rows_two * n_col
    span, share, cells = rows_one * rows_two, rank // n, depth // n
    dma = pltpu.SemaphoreType.DMA

    held, turned, whole_one, whole_two = linked(
        front_kernel,
        n_row,
        n_col,
        3,
        [(n, share, span), (depth, span), (n_one, rank), (n_two, rank)],
        [
            pltpu.VMEM((n, share, span), jnp.float32),
            dma((n,)),
            dma((n,)),
            dma((n_row,)),
            dma((n_row,)),
            dma((n_col,)),
            dma((n_col,)),
        ],
        tensor.reshape(span, depth),
        start_three.T,
        start_one,
        start_two,
    )
    cube = lax.all_to_all(turned.reshape(n, cells, span), both, split_axis=0, concat_axis=0, tiled=True)
    held = held.reshape(n_row, n_col, share, rows_one, rows_two).transpose(2, 0, 3, 1, 4)
    held = held.reshape(share, n_one, n_two)

    add = functools.partial(sum_all, n_row, n_col)
    (part,) = on_core(gram_one_kernel, [(n_one, n_one)], held, whole_two)
    gram_one = add("sum_gram", 1, part)
    basis_one, factor_one, part = on_core(
        mode_one_kernel, [(n_one, rank), (rank, n_one), (n_two, n_two)], gram_one, whole_one, held
    )
    gram_two = add("sum_gram", 1, part)
    own_a, own_b = rank // n_row, rank // n_col
    factor_two, blocks = on_core(
        functools.partial(mode_two_kernel, n_row, n_col),
        [(rank, n_two), (n, cells, own_a * own_b)],
        gram_two,
        whole_two,
        basis_one,
        cube,
        scratch=[(n_two, rank), (n_one * cells, n_two), (cells * rank, n_two)],
    )
    packed, count = (depth // 2, 2 * rank), depth // 2 // n_row
    factor_three, core = linked(
        tail_kernel,
        n_row,
        n_col,
        4,
        [(rank, depth), (own_a * own_b, rank)],
        [
            pltpu.VMEM((n, cells, own_a * own_b), jnp.float32),
            pltpu.VMEM(packed, jnp.float32),
            pltpu.VMEM(packed, jnp.float32),
            pltpu.VMEM((n_row, count, 2 * rank), jnp.float32),
            pltpu.VMEM((2, n_col, count, 2 * rank), jnp.float32),
            dma((n,)),
            dma((n,)),
            dma((n_row,)),
            dma((n_row,)),
            dma((2, n_col)),
            dma((2, n_col)),
            dma((n_row,)),
            dma((n_row,)),
        ],
        blocks,
        start_three.T,
    )
    factor_three = factor_three.T
    return (factor_one.T, factor_two.T, factor_three, core.reshape(own_a, own_b, rank).transpose(2, 0, 1))


def solution(mesh):
    n_row, n_col = mesh.shape["row"], mesh.shape["col"]
    n = n_row * n_col

    def on_device(tensor, start_one, start_two, start_three):
        rows_one, rows_two, depth = tensor.shape
        rank = start_three.shape[1]
        even = (
            rank % n == 0
            and depth % (2 * n_row * SUBLANES) == 0
            and depth % (n * SUBLANES) == 0
            and rows_one % SUBLANES == 0
            and rows_one * n_row == rows_two * n_col == LANES
            and rank * rank == n * LANES
        )
        if even:
            return shared(n_row, n_col, tensor, start_one, start_two, start_three)
        return general(tensor, start_one, start_two, start_three)

    return jax.shard_map(
        on_device,
        mesh=mesh,
        in_specs=(P("row", "col", None), P("row", None), P("col", None), P()),
        out_specs=(P(), P(), P(), P(None, "row", "col")),
        check_vma=False,
    )
```

profile of v0, /device:TPU:0, one launch (start us, length us, event | category | flops | bytes accessed | tf_op | source)
XLA Modules:
  0.0 192.9 jit_solution(11160749540751915967)
XLA Ops:
  0.6 18.1 %shard_map.75 = (f32[32,2,512]{2,1,0:T(2,128)}, f32[768,512]{1,0:T(8,128)}, f32[128,64]{1,0:T(8,128)}, f32[128,64]{1,0:T(8,128)}) custom-call(f32[512,768]{1,0:T(8,128)} %bitcast.16, f32[64,768]{1,0:T(8,128)} %bitcast.17, f32[16,64]{1,0:T(8,128)} %one_ref.1, f32[32,64]{1,0:T(8,128)} %two_ref.1), custom_call_target="tpu_custom_call" | custom-call | flops 1000000000 | bytes 10000000 | tf_op jit(solution)/shard_map/pallas_call | solution.py:479
  18.7 0.0 copy-start.1
  18.7 3.5 %all-to-all-start = ((f32[32,24,512]{2,1,0:T(8,128)}), f32[32,24,512]{2,1,0:T(8,128)S(1)}, u32[]{:S(2)}, u32[]{:S(2)}) async-start(f32[32,24,512]{2,1,0:T(8,128)} %bitcast.13), calls=%async_computation | async-start | bytes 3145728 | tf_op jit(solution)/shard_map/all_to_all | solution.py:519
  22.2 0.0 copy-done.1
  22.3 0.2 reshape.24
  22.5 0.3 copy.10
  22.8 0.9 reshape.25.held_ref
  23.8 2.2 %shard_map.76.refs_0_ = f32[128,128]{1,0:T(8,128)} custom-call(f32[2,128,128]{2,1,0:T(8,128)} %reshape.25.held_ref, f32[128,64]{1,0:T(8,128)} %get-tuple-element.16.start_ref), custom_call_target="tpu_custom_call" | custom-call | flops 2000000000 | bytes 2000000 | tf_op jit(solution)/shard_map/pallas_call | solution.py:237
  25.9 39.4 %sum_gram.2.gram_ref = f32[128,128]{1,0:T(8,128)} custom-call(f32[128,128]{1,0:T(8,128)} %shard_map.76.refs_0_), custom_call_target="tpu_custom_call" | custom-call | flops 1000000000 | bytes 10000000 | tf_op jit(solution)/shard_map/sum_gram/pallas_call | solution.py:314
  65.3 12.4 %shard_map.77 = (f32[128,64]{1,0:T(8,128)}, f32[64,128]{1,0:T(8,128)}, f32[128,128]{1,0:T(8,128)}) custom-call(f32[128,128]{1,0:T(8,128)} %sum_gram.2.gram_ref, f32[128,64]{1,0:T(8,128)} %get-tuple-element.17.start_ref, f32[2,128,128]{2,1,0:T(8,128)} %reshape.25.held_ref), custom_call_target="tpu_custom_call" | custom-call | flops 2000000000 | bytes 2000000 | tf_op jit(solution)/shard_map/pallas_call | solution.py:237
  77.8 13.7 %sum_gram.3.gram_ref = f32[128,128]{1,0:T(8,128)} custom-call(f32[128,128]{1,0:T(8,128)} %get-tuple-element.19.refs_0_), custom_call_target="tpu_custom_call" | custom-call | flops 1000000000 | bytes 10000000 | tf_op jit(solution)/shard_map/sum_gram/pallas_call | solution.py:314
  91.5 0.0 all-to-all-done.cube_ref
  91.5 0.0 copy-start
  91.5 1.1 copy-done
  92.6 16.0 %shard_map.78 = (f32[64,128]{1,0:T(8,128)}, f32[32,24,128]{2,1,0:T(8,128)}) custom-call(f32[128,128]{1,0:T(8,128)} %sum_gram.3.gram_ref, f32[128,64]{1,0:T(8,128)} %get-tuple-element.16.start_ref, f32[128,64]{1,0:T(8,128)} %get-tuple-element.20.one_ref, f32[32,24,512]{2,1,0:T(8,128)} %copy-done), custom_call_target="tpu_custom_call" | custom-call | flops 2000000000 | bytes 2000000 | tf_op jit(solution)/shard_map/pallas_call | solution.py:237
  108.6 81.3 %shard_map.79 = (f32[64,768]{1,0:T(8,128)}, f32[128,64]{1,0:T(8,128)}) custom-call(f32[32,24,128]{2,1,0:T(8,128)} %get-tuple-element.23.send_ref, f32[64,768]{1,0:T(8,128)} %bitcast.18), custom_call_target="tpu_custom_call" | custom-call | flops 1000000000 | bytes 10000000 | tf_op jit(solution)/shard_map/pallas_call | solution.py:479
  189.9 1.6 copy.13
  191.5 1.5 copy.14
Async XLA Ops:
  18.7 3.5 %copy-start.1 = (f32[32,2,512]{2,1,0:T(2,128)S(1)}, f32[32,2,512]{2,1,0:T(2,128)}, u32[]{:S(2)}) copy-start(f32[32,2,512]{2,1,0:T(2,128)} %get-tuple-element.15) | copy-start | bytes 393220
  18.7 72.7 %all-to-all-start = ((f32[32,24,512]{2,1,0:T(8,128)}), f32[32,24,512]{2,1,0:T(8,128)S(1)}, u32[]{:S(2)}, u32[]{:S(2)}) async-start(f32[32,24,512]{2,1,0:T(8,128)} %bitcast.13), calls=%async_computation | async-start | bytes 3145728 | tf_op jit(solution)/shard_map/all_to_all | solution.py:519
  91.5 1.1 copy-start
where the time goes:
time: 193 us
  Pallas kernels  183 us (95%)
  local copies, waits for them, and re-layouts  5.71 us (3%)
  starting transfers between devices  3.49 us (2%)
    pallas_call x2, Pallas kernels, linked(): pl.pallas_call(functools.partial(kernel, n_row, n_col), out_shape=outs, i...  99.4 us
    pallas_call x2, Pallas kernels, sum_all(): pl.pallas_call(functools.partial(sum_kernel, n_row, n_col), out_shape=jax...  53.1 us
    pallas_call x3, Pallas kernels, on_core(): pl.pallas_call(kernel, out_shape=outs, in_specs=[spec] * len(operands), o...  30.6 us
    unnamed x6, local copies, waits for them, and re-layouts  4.23 us
  transfers between devices with their start and end apart: 1, of which 0 were waited for; matrix products, arithmetic and copies ran while one was open for 1% of the time, Pallas kernels for 35%

commit v1 on v0

v1 whole, which is shorter than its diff:
```python
import functools
import math
import types

import jax
import jax.numpy as jnp
from jax import lax
from jax.experimental import pallas as pl
from jax.experimental.pallas import tpu as pltpu
from jax.sharding import PartitionSpec as P

STEPS = 4


HIGHEST = lax.Precision.HIGHEST
MESH = pl.DeviceIdType.MESH
SUBLANES = 8
LANES = 128


def product(left, right):
    return jnp.dot(left, right, precision=HIGHEST, preferred_element_type=jnp.float32)


def left_product(left, right):
    return lax.dot_general(
        left, right, (((0,), (0,)), ((), ())), precision=HIGHEST, preferred_element_type=jnp.float32
    )


def right_product(left, right):
    return lax.dot_general(
        left, right, (((1,), (1,)), ((), ())), precision=HIGHEST, preferred_element_type=jnp.float32
    )


def cross_product(left, right):
    return lax.dot_general(
        left, right, (((0,), (1,)), ((), ())), precision=HIGHEST, preferred_element_type=jnp.float32
    )


def orthonormal(matrix, inner):
    lower = jnp.linalg.cholesky(inner)
    return jax.scipy.linalg.solve_triangular(lower, matrix.T, lower=True).T


def settle(gram_whole, basis):
    for iteration in range(STEPS):
        image = product(gram_whole, basis)
        basis = orthonormal(image, left_product(image, image))
    return basis


def general(tensor, start_one, start_two, start_three):
    rows_one, rows_two, depth = tensor.shape
    rank = start_three.shape[1]
    flat = tensor.reshape(rows_one * rows_two, depth)
    contracted = cross_product(start_three, flat).reshape(rank, rows_one, rows_two)
    part_one = jnp.einsum("cij,jb->ibc", contracted, start_two, precision=HIGHEST).reshape(
        rows_one, rank * rank
    )
    slab_one = lax.psum_scatter(part_one, "col", scatter_dimension=1, tiled=True)
    slab_rows_one = lax.all_gather(slab_one, "row", axis=0, tiled=True)
    gram_one = lax.psum(right_product(slab_rows_one, slab_rows_one), "col")
    basis_one = settle(gram_one, lax.all_gather(start_one, "row", axis=0, tiled=True))
    own_one = lax.dynamic_slice_in_dim(basis_one, lax.axis_index("row") * rows_one, rows_one, 0)
    part_two = jnp.einsum("cij,ia->jac", contracted, own_one, precision=HIGHEST).reshape(
        rows_two, rank * rank
    )
    slab_two = lax.psum_scatter(part_two, "row", scatter_dimension=1, tiled=True)
    slab_rows_two = lax.all_gather(slab_two, "col", axis=0, tiled=True)
    gram_two = lax.psum(right_product(slab_rows_two, slab_rows_two), "row")
    basis_two = settle(gram_two, lax.all_gather(start_two, "col", axis=0, tiled=True))
    own_two = lax.dynamic_slice_in_dim(basis_two, lax.axis_index("col") * rows_two, rows_two, 0)
    received = lax.all_to_all(tensor, "row", split_axis=2, concat_axis=0, tiled=True)
    count, items, cells = received.shape
    merged = left_product(basis_one, received.reshape(count, items * cells))
    mixed = merged.reshape(rank, items, cells)
    part_three = jnp.einsum("ajk,jb->kba", mixed, own_two, precision=HIGHEST)
    cells_here = part_three.shape[0]
    slab_three = lax.psum_scatter(
        part_three.reshape(cells_here, rank * rank), "col", scatter_dimension=1, tiled=True
    )
    gram_part_three = right_product(slab_three, lax.all_gather(slab_three, "row", axis=0, tiled=True))
    gram_three = lax.psum(gram_part_three, "col")
    basis_three = start_three
    own_three = start_three
    for iteration in range(STEPS):
        image = product(gram_three, basis_three)
        inner = lax.psum(left_product(image, image), "row")
        own_three = orthonormal(image, inner)
        basis_three = lax.all_gather(own_three, "row", axis=0, tiled=True)
    core_part = left_product(own_three, slab_three)
    core_part = core_part.reshape(rank, core_part.shape[1] // rank, rank)
    core = lax.psum_scatter(core_part, "row", scatter_dimension=2, tiled=True).transpose(0, 2, 1)
    factor_one = basis_one * math.sqrt(basis_one.shape[0])
    factor_two = basis_two * math.sqrt(basis_two.shape[0])
    factor_three = basis_three * math.sqrt(basis_three.shape[0])
    return (factor_one, factor_two, factor_three, core)


def inverse_factor(inner):
    n = inner.shape[0]
    groups = n // SUBLANES
    eye = (
        lax.broadcasted_iota(jnp.int32, (n, n), 0) == lax.broadcasted_iota(jnp.int32, (n, n), 1)
    ).astype(jnp.float32)
    whole = jnp.concatenate([inner, eye], axis=1)
    width = whole.shape[1]
    rows = [whole[g * SUBLANES : (g + 1) * SUBLANES] for g in range(groups)]
    sub = lax.broadcasted_iota(jnp.int32, (SUBLANES, width), 0)
    pivots = [None] * n
    shape = (SUBLANES, width)
    for base in range(groups):
        columns = [
            [jnp.broadcast_to(rows[g][:, k : k + 1], shape) for g in range(base, groups)]
            for k in range(base * SUBLANES, (base + 1) * SUBLANES)
        ]
        for t in range(SUBLANES):
            pivot = jnp.broadcast_to(columns[t][0][t : t + 1, :], shape)
            scale = 1.0 / pivot
            pivots[base * SUBLANES + t] = pivot
            row = jnp.broadcast_to(rows[base][t : t + 1, :], shape)
            heads = [
                jnp.broadcast_to(columns[s][0][t : t + 1, :], shape) for s in range(t + 1, SUBLANES)
            ]
            for g in range(base, groups):
                factor = columns[t][g - base] * scale
                if g == base:
                    factor = jnp.where(sub > t, factor, 0.0)
                rows[g] = rows[g] - factor * row
                for s in range(t + 1, SUBLANES):
                    columns[s][g - base] = columns[s][g - base] - factor * heads[s - t - 1]
    out = []
    for g in range(groups):
        held = pivots[g * SUBLANES]
        for t in range(1, SUBLANES):
            held = jnp.where(sub == t, pivots[g * SUBLANES + t], held)
        out.append(rows[g] * lax.rsqrt(held))
    return jnp.concatenate(out, axis=0)[:, n:]


def lane_groups(width):
    return lax.div(lax.broadcasted_iota(jnp.int32, (1, LANES), 1), width)


def shifted(value, amount):
    amount = amount % LANES
    return value if amount == 0 else pltpu.roll(value, amount, 1)


def settle_turned(gram_ref, basis_ref):
    def one(_, carry):
        image = product(basis_ref[...], gram_ref[...])
        basis_ref[...] = product(inverse_factor(right_product(image, image)), image)
        return carry

    lax.fori_loop(0, STEPS, one, 0)


def aligned(start, count, multiple=SUBLANES):
    return pl.ds(pl.multiple_of(start, multiple), count)


def remote(source, target, send, recv, row, col):
    return pltpu.make_async_remote_copy(
        src_ref=source, dst_ref=target, send_sem=send, recv_sem=recv, device_id=(row, col), device_id_type=MESH
    )


def start_all(made):
    for copy in made:
        copy.start()
    return made


def greet_all(n_row, n_col):
    n = n_row * n_col
    me = lax.axis_index("row") * n_col + lax.axis_index("col")
    barrier = pltpu.get_barrier_semaphore()

    def one(d, carry):
        peer = lax.rem(me + d, n)
        pl.semaphore_signal(
            barrier, inc=1, device_id=(peer // n_col, lax.rem(peer, n_col)), device_id_type=MESH
        )
        return carry

    lax.fori_loop(1, n, one, 0)
    return barrier


def chain_scratch(n_row, n_col, rows_one, rows_two, depth, rank):
    n, chips, plane = n_row * n_col, n_row * n_col // 2, n_row // 2
    half, blocks, chunk, n_one, n_two = depth // 2, rank // chips, rank // plane, LANES, LANES
    share = rank // n

    def buffer(*shape):
        return pltpu.VMEM(shape, jnp.float32)

    def dma(*shape):
        return pltpu.SemaphoreType.DMA(shape)

    return dict(
        parted=buffer(n * SUBLANES, LANES),
        held=buffer(n * SUBLANES, LANES),
        faces=buffer(share * n_one, n_two),
        turned=buffer(share, n_two, n_one),
        all_one=buffer(n_one, rank),
        all_two=buffer(n_two, rank),
        gram_part=buffer(2, LANES, LANES),
        gram_parts=buffer(2, n_row, LANES // n_row, LANES),
        gram_planes=buffer(2, n_col, LANES // n_row, LANES),
        gram_sum=buffer(2, LANES, LANES),
        basis_one=buffer(rank, n_one),
        basis_two=buffer(rank, n_two),
        block=buffer(half // LANES, n_one, SUBLANES, LANES),
        mixed=buffer(half // LANES, rank, SUBLANES, LANES),
        joined=buffer(half // LANES, blocks, n_two, LANES),
        slab=buffer(blocks * rank, half),
        image=buffer(STEPS + 1, rank, half),
        cross_own=buffer(STEPS, rank, blocks * rank),
        cross_pair=buffer(STEPS, rank, blocks * rank),
        inner_own=buffer(STEPS + 1, rank, rank),
        inner_pair=buffer(STEPS + 1, rank, rank),
        image_part=buffer(STEPS, rank, half),
        image_parts=buffer(STEPS, plane, chunk, half),
        image_planes=buffer(STEPS, n_col, chunk, half),
        last=buffer(rank, half),
        core_own=buffer(blocks * rank, rank),
        core_pair=buffer(blocks * rank, rank),
        core_sum=buffer(blocks, rank, rank),
        core_all=buffer(n_col * blocks, rank // n_col, rank),
        s_held=dma(n), r_held=dma(n),
        s_one=dma(n_row), r_one=dma(n_row),
        s_two=dma(n_col), r_two=dma(n_col),
        s_block=dma(half // LANES, n_row), r_block=dma(half // LANES, n_row),
        own=dma(half // LANES),
        s_gram_row=dma(2, n_row), r_gram_row=dma(2, n_row),
        s_gram_col=dma(2, n_col), r_gram_col=dma(2, n_col),
        s_gram_all=dma(2, n_row), r_gram_all=dma(2, n_row),
        s_mixed=dma(chips), r_mixed=dma(chips),
        s_cross=dma(STEPS), r_cross=dma(STEPS),
        s_inner=dma(STEPS + 1), r_inner=dma(STEPS + 1),
        s_image_row=dma(STEPS, plane), r_image_row=dma(STEPS, plane),
        s_image_col=dma(STEPS, n_col), r_image_col=dma(STEPS, n_col),
        s_image_all=dma(STEPS, plane), r_image_all=dma(STEPS, plane),
        s_last=dma(2), r_last=dma(2),
        s_core=dma(n_col), r_core=dma(n_col),
    )


def chain_kernel(n_row, n_col, names, t_ref, v_ref, one_ref, two_ref, f1_ref, f2_ref, last_ref, linv_ref, piece_ref, *refs):
    g = types.SimpleNamespace(**dict(zip(names, refs)))
    row, col = lax.axis_index("row"), lax.axis_index("col")
    n, plane, chips = n_row * n_col, n_row // 2, n_row * n_col // 2
    me, chip, core = row * n_col + col, row // 2, lax.rem(row, 2)
    other = row + 1 - 2 * core
    rows_one, rows_two, depth = t_ref.shape
    rank, half = v_ref.shape[0], depth // 2
    share, tiles = rank // n, rows_one * rows_two // LANES
    n_one = n_two = LANES

    def row_peer(d):
        return lax.rem(row + d, n_row)

    def col_peer(d):
        return lax.rem(col + d, n_col)

    def plane_peer(d):
        return lax.rem(chip + d, plane)

    barrier = greet_all(n_row, n_col)
    contracted = right_product(v_ref[...], t_ref[...].reshape(rows_one * rows_two, depth))
    for tile in range(tiles):
        g.parted[pl.ds(tile, rank, stride=tiles), :] = contracted[:, tile * LANES : (tile + 1) * LANES]
    pl.semaphore_wait(barrier, n - 1)
    place = col * n_row + row

    def held_copy(d):
        peer = lax.rem(me + d, n)
        return remote(
            g.parted.at[aligned(peer * SUBLANES, SUBLANES), :],
            g.held.at[aligned(place * SUBLANES, SUBLANES), :],
            g.s_held.at[d], g.r_held.at[d], peer // n_col, lax.rem(peer, n_col),
        )

    def held_start(d, carry):
        held_copy(d).start()
        return carry

    def held_wait(d, carry):
        held_copy(d).wait()
        return carry

    lax.fori_loop(1, n, held_start, 0)
    own_one, own_two = aligned(row * rows_one, rows_one), aligned(col * rows_two, rows_two)
    starts = start_all(
        [remote(two_ref, g.all_two.at[own_two, :], g.s_two.at[d], g.r_two.at[d], row, col_peer(d)) for d in range(1, n_col)]
        + [remote(one_ref, g.all_one.at[own_one, :], g.s_one.at[d], g.r_one.at[d], row_peer(d), col) for d in range(1, n_row)]
    )

    portions = half // LANES

    def block_source(which, peer):
        return t_ref.at[
            :,
            aligned(peer // 2 * SUBLANES, SUBLANES),
            aligned(lax.rem(peer, 2) * half + which * LANES, LANES, LANES),
        ]

    def block_target(which):
        return g.block.at[which, pl.ds(row * rows_one, rows_one)]

    def block_copies(which):
        return [
            remote(
                block_source(which, row_peer(d)), block_target(which),
                g.s_block.at[which, d], g.r_block.at[which, d], row_peer(d), col,
            )
            for d in range(1, n_row)
        ]

    bulk = start_all(block_copies(0))
    kept = start_all(
        [pltpu.make_async_copy(block_source(w, row), block_target(w), g.own.at[w]) for w in range(portions)]
    )
    g.held[aligned(place * SUBLANES, SUBLANES), :] = g.parted[aligned(me * SUBLANES, SUBLANES), :]
    g.all_one[own_one, :] = one_ref[...]
    g.all_two[own_two, :] = two_ref[...]
    g.image[0] = v_ref[:, aligned(core * half, half, LANES)]
    linv_ref[...] = unit(rank)
    for copy in starts:
        copy.wait()
    lax.fori_loop(1, n, held_wait, 0)
    group = lane_groups(rows_two)
    for c in range(share):
        for tile in range(tiles):
            blocks = [
                g.held[pl.ds(q * n_row * SUBLANES + c * tiles + tile, n_row, stride=SUBLANES), :] for q in range(n_col)
            ]
            for s in range(n_col):
                line = shifted(blocks[0], -s * rows_two)
                for q in range(1, n_col):
                    line = jnp.where(group == q, shifted(blocks[q], (q - s) * rows_two), line)
                g.faces[pl.ds(c * n_one + tile * n_col + s, n_row, stride=rows_one), :] = line

    count = LANES // n_row
    own_rows = aligned(row * count, count)

    def gram_first(w):
        return start_all(
            [
                remote(
                    g.gram_part.at[w, aligned(row_peer(d) * count, count), :], g.gram_parts.at[w, d],
                    g.s_gram_row.at[w, d], g.r_gram_row.at[w, d], row_peer(d), col,
                )
                for d in range(1, n_row)
            ]
        )

    def gram_second(w, first):
        total = g.gram_part[w, own_rows, :]
        for d in range(1, n_row):
            first[d - 1].wait_recv()
            total = total + g.gram_parts[w, d]
        g.gram_planes[w, col] = total
        return start_all(
            [
                remote(
                    g.gram_planes.at[w, col], g.gram_planes.at[w, col],
                    g.s_gram_col.at[w, d], g.r_gram_col.at[w, d], row, col_peer(d),
                )
                for d in range(1, n_col)
            ]
        )

    def gram_third(w, second):
        for copy in second:
            copy.wait_recv()
        total = g.gram_planes[w, 0]
        for q in range(1, n_col):
            total = total + g.gram_planes[w, q]
        g.gram_sum[w, own_rows, :] = total
        return start_all(
            [
                remote(
                    g.gram_sum.at[w, own_rows, :], g.gram_sum.at[w, own_rows, :],
                    g.s_gram_all.at[w, d], g.r_gram_all.at[w, d], row_peer(d), col,
                )
                for d in range(1, n_row)
            ]
        )

    def gram_end(first, second, third):
        for copy in third:
            copy.wait_recv()
        for copy in first + second + third:
            copy.wait_send()

    def self_gram(slabs):
        total = right_product(slabs[0], slabs[0])
        for slab in slabs[1:]:
            total = total + right_product(slab, slab)
        return total

    g.gram_part[0] = self_gram(
        [product(g.faces[c * n_one : (c + 1) * n_one, :], g.all_two[...]) for c in range(share)]
    )
    first = gram_first(0)
    for c in range(share):
        g.turned[c] = g.faces[c * n_one : (c + 1) * n_one, :].T
    g.basis_one[...] = g.all_one[...].T
    g.basis_two[...] = g.all_two[...].T
    second = gram_second(0, first)
    third = gram_third(0, second)
    gram_end(first, second, third)
    for which in range(1, portions):
        bulk = bulk + start_all(block_copies(which))
    settle_turned(g.gram_sum.at[0], g.basis_one)
    basis_one = g.basis_one[...]

    g.gram_part[1] = self_gram([right_product(g.turned[c], basis_one) for c in range(share)])
    first = gram_first(1)
    f1_ref[...] = basis_one * math.sqrt(n_one)
    for copy in bulk:
        copy.wait()
    for copy in kept:
        copy.wait()
    flat_block = g.block.reshape(portions * n_one * SUBLANES, LANES)
    flat_mixed = g.mixed.reshape(portions * rank * SUBLANES, LANES)
    for s in range(SUBLANES):
        face = [flat_block[pl.ds(w * n_one * SUBLANES + s, n_one, stride=SUBLANES), :] for w in range(portions)]
        face = product(basis_one, jnp.concatenate(face, axis=1))
        for w in range(portions):
            flat_mixed[pl.ds(w * rank * SUBLANES + s, rank, stride=SUBLANES), :] = face[:, w * LANES : (w + 1) * LANES]
    second = gram_second(1, first)
    third = gram_third(1, second)
    gram_end(first, second, third)

    pieces = rank // chips
    place = chip * n_col + col
    lines = aligned(col * rows_two + chip * SUBLANES, SUBLANES)
    moved = []
    for d in range(1, chips):
        peer = lax.rem(place + d, chips)
        moved.append(
            remote(
                g.mixed.at[:, pl.ds(peer * pieces, pieces)], g.joined.at[:, :, lines, :],
                g.s_mixed.at[d], g.r_mixed.at[d], peer // n_col * 2 + core, lax.rem(peer, n_col),
            )
        )
    start_all(moved)
    g.joined[:, :, lines, :] = g.mixed[:, pl.ds(place * pieces, pieces)]
    settle_turned(g.gram_sum.at[1], g.basis_two)
    basis_two = g.basis_two[...]
    f2_ref[...] = basis_two * math.sqrt(n_two)
    for copy in moved:
        copy.wait()
    for a in range(pieces):
        g.slab[a * rank : (a + 1) * rank, :] = product(
            basis_two, jnp.concatenate([g.joined[w, a] for w in range(portions)], axis=1)
        )

    chunk = rank // plane
    own_chunk = aligned(chip * chunk, chunk)

    def pair(source, target, send, recv):
        copy = remote(source, target, send, recv, other, col)
        copy.start()
        return copy

    def one(step, carry):
        iterate = product(linv_ref[...], g.image[step])
        g.cross_own[step] = right_product(iterate, g.slab[...])
        crossing = pair(g.cross_own.at[step], g.cross_pair.at[step], g.s_cross.at[step], g.r_cross.at[step])
        g.inner_own[step] = right_product(iterate, iterate)
        meeting = pair(g.inner_own.at[step], g.inner_pair.at[step], g.s_inner.at[step], g.r_inner.at[step])
        crossing.wait()
        g.image_part[step] = product(g.cross_own[step] + g.cross_pair[step], g.slab[...])
        first = start_all(
            [
                remote(
                    g.image_part.at[step, aligned(plane_peer(d) * chunk, chunk), :], g.image_parts.at[step, d],
                    g.s_image_row.at[step, d], g.r_image_row.at[step, d], plane_peer(d) * 2 + core, col,
                )
                for d in range(1, plane)
            ]
        )
        meeting.wait()
        total = g.image_part[step, own_chunk, :]
        for d in range(1, plane):
            first[d - 1].wait_recv()
            total = total + g.image_parts[step, d]
        g.image_planes[step, col] = total
        second = start_all(
            [
                remote(
                    g.image_planes.at[step, col], g.image_planes.at[step, col],
                    g.s_image_col.at[step, d], g.r_image_col.at[step, d], row, col_peer(d),
                )
                for d in range(1, n_col)
            ]
        )
        inverse = inverse_factor(g.inner_own[step] + g.inner_pair[step])
        linv_ref[...] = jnp.where(step == 0, unit(rank), inverse)
        for copy in second:
            copy.wait_recv()
        total = g.image_planes[step, 0]
        for q in range(1, n_col):
            total = total + g.image_planes[step, q]
        g.image[step + 1, own_chunk, :] = total
        third = start_all(
            [
                remote(
                    g.image.at[step + 1, own_chunk, :], g.image.at[step + 1, own_chunk, :],
                    g.s_image_all.at[step, d], g.r_image_all.at[step, d], plane_peer(d) * 2 + core, col,
                )
                for d in range(1, plane)
            ]
        )
        for copy in third:
            copy.wait_recv()
        for copy in first + second + third:
            copy.wait_send()
        return carry

    lax.fori_loop(0, STEPS, one, 0)
    iterate = product(linv_ref[...], g.image[STEPS])
    g.core_own[...] = right_product(g.slab[...], iterate)
    crossing = pair(g.core_own, g.core_pair, g.s_last.at[0], g.r_last.at[0])
    g.inner_own[STEPS] = right_product(iterate, iterate)
    meeting = pair(g.inner_own.at[STEPS], g.inner_pair.at[STEPS], g.s_inner.at[STEPS], g.r_inner.at[STEPS])
    mine = aligned(core * half, half, LANES)
    g.last[...] = iterate
    last_ref[:, mine] = iterate
    lasting = pair(g.last, last_ref.at[:, mine], g.s_last.at[1], g.r_last.at[1])
    crossing.wait()
    g.core_sum[...] = (g.core_own[...] + g.core_pair[...]).reshape(pieces, rank, rank)
    own_b = rank // n_col
    own_pieces = pl.ds(col * pieces, pieces)
    moved = start_all(
        [
            remote(
                g.core_sum.at[:, aligned(col_peer(d) * own_b, own_b), :], g.core_all.at[own_pieces],
                g.s_core.at[d], g.r_core.at[d], row, col_peer(d),
            )
            for d in range(1, n_col)
        ]
    )
    g.core_all[own_pieces] = g.core_sum[:, aligned(col * own_b, own_b), :]
    meeting.wait()
    linv_ref[...] = inverse_factor(g.inner_own[STEPS] + g.inner_pair[STEPS])
    lasting.wait()
    for copy in moved:
        copy.wait()
    own_a = piece_ref.shape[0]
    piece_ref[...] = g.core_all[pl.ds(core * own_a, own_a)]


def finish_kernel(one_ref, two_ref, last_ref, linv_ref, piece_ref, f1_ref, f2_ref, f3_ref, core_ref):
    f1_ref[...] = one_ref[...]
    f2_ref[...] = two_ref[...]
    linv = linv_ref[...]
    f3_ref[...] = product(linv, last_ref[...]) * math.sqrt(last_ref.shape[1])
    core_ref[...] = right_product(piece_ref[...].reshape(core_ref.shape), linv)


def unit(size):
    shape = (size, size)
    return (lax.broadcasted_iota(jnp.int32, shape, 0) == lax.broadcasted_iota(jnp.int32, shape, 1)).astype(jnp.float32)


def shared(n_row, n_col, tensor, start_one, start_two, start_three):
    rows_one, rows_two, depth = tensor.shape
    rank = start_three.shape[1]
    own_a, own_b = rank // n_row, rank // n_col
    spec = pl.BlockSpec(memory_space=pltpu.VMEM)
    scratch = chain_scratch(n_row, n_col, rows_one, rows_two, depth, rank)

    def outs(*shapes):
        return [jax.ShapeDtypeStruct(shape, jnp.float32) for shape in shapes]

    chained = pl.pallas_call(
        functools.partial(chain_kernel, n_row, n_col, tuple(scratch)),
        out_shape=outs((rank, LANES), (rank, LANES), (rank, depth), (rank, rank), (own_a, own_b, rank)),
        in_specs=[spec] * 4,
        out_specs=[spec] * 5,
        scratch_shapes=list(scratch.values()),
        compiler_params=pltpu.CompilerParams(
            collective_id=1, has_side_effects=True, vmem_limit_bytes=48 * 2**20
        ),
        cost_estimate=pl.CostEstimate(flops=10**9, bytes_accessed=10**7, transcendentals=0),
        name="chain",
    )(tensor, start_three.T, start_one, start_two)
    factor_one, factor_two, factor_three, core = pl.pallas_call(
        finish_kernel,
        out_shape=outs((rank, LANES), (rank, LANES), (rank, depth), (own_a * own_b, rank)),
        in_specs=[spec] * 5,
        out_specs=[spec] * 4,
        cost_estimate=pl.CostEstimate(flops=10**7, bytes_accessed=10**6, transcendentals=0),
        name="finish",
    )(*chained)
    return (factor_one.T, factor_two.T, factor_three.T, core.reshape(own_a, own_b, rank).transpose(2, 0, 1))


def solution(mesh):
    n_row, n_col = mesh.shape["row"], mesh.shape["col"]
    n = n_row * n_col

    def on_device(tensor, start_one, start_two, start_three):
        rows_one, rows_two, depth = tensor.shape
        rank = start_three.shape[1]
        plane, span = n_row // 2, rows_one * rows_two
        even = (
            n_row % 2 == 0
            and rows_one * n_row == rows_two * n_col == LANES
            and rows_two == plane * SUBLANES
            and rows_one % SUBLANES == 0
            and depth % (2 * LANES) == 0
            and rank % (plane * SUBLANES) == 0
            and rank % (n_col * SUBLANES) == 0
            and rank % n == 0
            and rank // n * (span // LANES) == SUBLANES
        )
        if even:
            return shared(n_row, n_col, tensor, start_one, start_two, start_three)
        return general(tensor, start_one, start_two, start_three)

    return jax.shard_map(
        on_device,
        mesh=mesh,
        in_specs=(P("row", "col", None), P("row", None), P("col", None), P()),
        out_specs=(P(), P(), P(), P(None, "row", "col")),
        check_vma=False,
    )
```

time: 193 us -> 138 us (0.72)
  Pallas kernels: 183 us -> 130 us
  starting transfers between devices: 3.49 us -> 0 us
    pallas_call x7 -> x2, Pallas kernels: 183 us -> 130 us  [the longest x1 128 us: shared(): pl.pallas_call(functools.partial(chain_kernel, n_row, n_col, tuple(scratc...]
    all_to_all x1 -> x0, starting transfers between devices: 3.49 us -> none  [shared(): lax.all_to_all(turned.reshape(n, cells, span), both, split_axis=0, concat...]
    unnamed x6 -> x18, local copies, waits for them, and re-layouts: 4.23 us -> 6.85 us
  transfers between devices with their start and end apart: 1 -> 0, of which waited for: 0 -> 0; matrix products, arithmetic and copies ran while one was open for 1% -> 0% of each run, Pallas kernels for 35% -> 0%
where the time goes in v1:
time: 138 us
  Pallas kernels  130 us (94%)
  local copies, waits for them, and re-layouts  6.85 us (5%)
    pallas_call x1, Pallas kernels, shared(): pl.pallas_call(functools.partial(chain_kernel, n_row, n_col, tuple(scratc...  128 us
    unnamed x18, local copies, waits for them, and re-layouts  6.85 us

profile of v1, /device:TPU:0, one launch (start us, length us, event | category | flops | bytes accessed | tf_op | source)
XLA Modules:
  0.0 137.5 jit_solution(10366177333637980857)
XLA Ops:
  0.6 0.0 copy-start.5
  0.6 1.4 %copy-done.5 = f32[16,32,768]{2,1,0:T(8,128)S(1)} copy-done((f32[16,32,768]{2,1,0:T(8,128)S(1)}, f32[16,32,768]{2,1,0:T(8,128)}, u32[]{:S(2)}) %copy-start.5) | copy-done | bytes 1572888
  2.0 0.0 copy-start.6
  2.0 0.9 copy-done.6
  3.0 0.0 copy-start.7
  3.0 0.7 copy-done.7
  3.7 0.0 copy-start.8
  3.7 0.7 copy-done.8
  4.4 127.9 %chain.1 = (f32[64,128]{1,0:T(8,128)S(1)}, f32[64,128]{1,0:T(8,128)S(1)}, f32[64,768]{1,0:T(8,128)S(1)}, f32[64,64]{1,0:T(8,128)S(1)}, f32[8,16,64]{2,1,0:T(8,128)S(1)}) custom-call(f32[16,32,768]{2,1,0:T(8,128)S(1)} %copy-done.5, f32[64,768]{1,0:T(8,128)S(1)} %bitcast.7, f32[16,64]{1,0:T(8,128)S(1)} %copy-done.8, f32[32,64]{1,0:T(8,128)S(1)} %copy-done.7), custom_call_target="tpu_custom_call" | custom-call | flops 1000000000 | bytes 10000000 | tf_op jit(solution)/shard_map/chain/pallas_call | solution.py:585
  132.3 0.0 copy-start
  132.3 0.7 copy-done
  133.0 0.0 copy-start.1
  133.0 0.6 copy-done.1
  133.6 0.0 copy-start.2
  133.6 0.6 copy-done.2
  134.2 0.0 copy-start.3
  134.2 0.6 copy-done.3
  134.8 0.0 copy-start.4
  134.8 0.6 copy-done.4
  135.4 2.1 %finish.1 = (f32[64,128]{1,0:T(8,128)}, f32[64,128]{1,0:T(8,128)}, f32[64,768]{1,0:T(8,128)}, f32[128,64]{1,0:T(8,128)}) custom-call(f32[64,128]{1,0:T(8,128)} %copy-done.2, f32[64,128]{1,0:T(8,128)} %copy-done.3, f32[64,768]{1,0:T(8,128)} %copy-done, f32[64,64]{1,0:T(8,128)} %copy-done.4, f32[8,16,64]{2,1,0:T(8,128)} %copy-done.1), custom_call_target="tpu_custom_call" | custom-call | flops 10000000 | bytes 1000000 | tf_op jit(solution)/shard_map/finish/pallas_call | solution.py:597
Async XLA Ops:
  0.6 1.4 %copy-start.5 = (f32[16,32,768]{2,1,0:T(8,128)S(1)}, f32[16,32,768]{2,1,0:T(8,128)}, u32[]{:S(2)}) copy-start(f32[16,32,768]{2,1,0:T(8,128)} %t_ref.1) | copy-start | bytes 4718596
  2.0 0.9 copy-start.6
  3.0 0.7 copy-start.7
  3.7 0.7 copy-start.8
  132.3 0.7 copy-start
  133.0 0.6 copy-start.1
  133.6 0.6 copy-start.2
  134.2 0.6 copy-start.3
  134.8 0.6 copy-start.4

commit v2 on v1

v2 whole, which is shorter than its diff:
```python
import functools
import math
import types

import jax
import jax.numpy as jnp
from jax import lax
from jax.experimental import pallas as pl
from jax.experimental.pallas import tpu as pltpu
from jax.sharding import PartitionSpec as P

STEPS = 4


HIGHEST = lax.Precision.HIGHEST
MESH = pl.DeviceIdType.MESH
SUBLANES = 8
LANES = 128


def product(left, right):
    return jnp.dot(left, right, precision=HIGHEST, preferred_element_type=jnp.float32)


def left_product(left, right):
    return lax.dot_general(
        left, right, (((0,), (0,)), ((), ())), precision=HIGHEST, preferred_element_type=jnp.float32
    )


def right_product(left, right):
    return lax.dot_general(
        left, right, (((1,), (1,)), ((), ())), precision=HIGHEST, preferred_element_type=jnp.float32
    )


def cross_product(left, right):
    return lax.dot_general(
        left, right, (((0,), (1,)), ((), ())), precision=HIGHEST, preferred_element_type=jnp.float32
    )


def orthonormal(matrix, inner):
    lower = jnp.linalg.cholesky(inner)
    return jax.scipy.linalg.solve_triangular(lower, matrix.T, lower=True).T


def settle(gram_whole, basis):
    for iteration in range(STEPS):
        image = product(gram_whole, basis)
        basis = orthonormal(image, left_product(image, image))
    return basis


def general(tensor, start_one, start_two, start_three):
    rows_one, rows_two, depth = tensor.shape
    rank = start_three.shape[1]
    flat = tensor.reshape(rows_one * rows_two, depth)
    contracted = cross_product(start_three, flat).reshape(rank, rows_one, rows_two)
    part_one = jnp.einsum("cij,jb->ibc", contracted, start_two, precision=HIGHEST).reshape(
        rows_one, rank * rank
    )
    slab_one = lax.psum_scatter(part_one, "col", scatter_dimension=1, tiled=True)
    slab_rows_one = lax.all_gather(slab_one, "row", axis=0, tiled=True)
    gram_one = lax.psum(right_product(slab_rows_one, slab_rows_one), "col")
    basis_one = settle(gram_one, lax.all_gather(start_one, "row", axis=0, tiled=True))
    own_one = lax.dynamic_slice_in_dim(basis_one, lax.axis_index("row") * rows_one, rows_one, 0)
    part_two = jnp.einsum("cij,ia->jac", contracted, own_one, precision=HIGHEST).reshape(
        rows_two, rank * rank
    )
    slab_two = lax.psum_scatter(part_two, "row", scatter_dimension=1, tiled=True)
    slab_rows_two = lax.all_gather(slab_two, "col", axis=0, tiled=True)
    gram_two = lax.psum(right_product(slab_rows_two, slab_rows_two), "row")
    basis_two = settle(gram_two, lax.all_gather(start_two, "col", axis=0, tiled=True))
    own_two = lax.dynamic_slice_in_dim(basis_two, lax.axis_index("col") * rows_two, rows_two, 0)
    received = lax.all_to_all(tensor, "row", split_axis=2, concat_axis=0, tiled=True)
    count, items, cells = received.shape
    merged = left_product(basis_one, received.reshape(count, items * cells))
    mixed = merged.reshape(rank, items, cells)
    part_three = jnp.einsum("ajk,jb->kba", mixed, own_two, precision=HIGHEST)
    cells_here = part_three.shape[0]
    slab_three = lax.psum_scatter(
        part_three.reshape(cells_here, rank * rank), "col", scatter_dimension=1, tiled=True
    )
    gram_part_three = right_product(slab_three, lax.all_gather(slab_three, "row", axis=0, tiled=True))
    gram_three = lax.psum(gram_part_three, "col")
    basis_three = start_three
    own_three = start_three
    for iteration in range(STEPS):
        image = product(gram_three, basis_three)
        inner = lax.psum(left_product(image, image), "row")
        own_three = orthonormal(image, inner)
        basis_three = lax.all_gather(own_three, "row", axis=0, tiled=True)
    core_part = left_product(own_three, slab_three)
    core_part = core_part.reshape(rank, core_part.shape[1] // rank, rank)
    core = lax.psum_scatter(core_part, "row", scatter_dimension=2, tiled=True).transpose(0, 2, 1)
    factor_one = basis_one * math.sqrt(basis_one.shape[0])
    factor_two = basis_two * math.sqrt(basis_two.shape[0])
    factor_three = basis_three * math.sqrt(basis_three.shape[0])
    return (factor_one, factor_two, factor_three, core)


def inverse_factor(inner):
    n = inner.shape[0]
    groups = n // SUBLANES
    eye = (
        lax.broadcasted_iota(jnp.int32, (n, n), 0) == lax.broadcasted_iota(jnp.int32, (n, n), 1)
    ).astype(jnp.float32)
    whole = jnp.concatenate([inner, eye], axis=1)
    width = whole.shape[1]
    rows = [whole[g * SUBLANES : (g + 1) * SUBLANES] for g in range(groups)]
    sub = lax.broadcasted_iota(jnp.int32, (SUBLANES, width), 0)
    pivots = [None] * n
    shape = (SUBLANES, width)
    for base in range(groups):
        columns = [
            [jnp.broadcast_to(rows[g][:, k : k + 1], shape) for g in range(base, groups)]
            for k in range(base * SUBLANES, (base + 1) * SUBLANES)
        ]
        for t in range(SUBLANES):
            pivot = jnp.broadcast_to(columns[t][0][t : t + 1, :], shape)
            scale = 1.0 / pivot
            pivots[base * SUBLANES + t] = pivot
            row = jnp.broadcast_to(rows[base][t : t + 1, :], shape)
            heads = [
                jnp.broadcast_to(columns[s][0][t : t + 1, :], shape) for s in range(t + 1, SUBLANES)
            ]
            for g in range(base, groups):
                factor = columns[t][g - base] * scale
                if g == base:
                    factor = jnp.where(sub > t, factor, 0.0)
                rows[g] = rows[g] - factor * row
                for s in range(t + 1, SUBLANES):
                    columns[s][g - base] = columns[s][g - base] - factor * heads[s - t - 1]
    out = []
    for g in range(groups):
        held = pivots[g * SUBLANES]
        for t in range(1, SUBLANES):
            held = jnp.where(sub == t, pivots[g * SUBLANES + t], held)
        out.append(rows[g] * lax.rsqrt(held))
    return jnp.concatenate(out, axis=0)[:, n:]


def lane_groups(width):
    return lax.div(lax.broadcasted_iota(jnp.int32, (1, LANES), 1), width)


def shifted(value, amount):
    amount = amount % LANES
    return value if amount == 0 else pltpu.roll(value, amount, 1)


def settle_turned(gram_ref, basis_ref):
    basis_ref[...] = product(basis_ref[...], gram_ref[...])

    def one(_, carry):
        image = basis_ref[...]
        further = product(image, gram_ref[...])
        basis_ref[...] = product(inverse_factor(right_product(image, image)), further)
        return carry

    lax.fori_loop(0, STEPS - 1, one, 0)
    image = basis_ref[...]
    basis_ref[...] = product(inverse_factor(right_product(image, image)), image)


def aligned(start, count, multiple=SUBLANES):
    return pl.ds(pl.multiple_of(start, multiple), count)


def remote(source, target, sems, row, col):
    return pltpu.make_async_remote_copy(
        src_ref=source, dst_ref=target, send_sem=sems[0], recv_sem=sems[1], device_id=(row, col), device_id_type=MESH
    )


def start_all(made):
    for copy in made:
        copy.start()


def wait_bytes(ref, sem):
    pltpu.make_async_copy(ref, ref, sem).wait()


def chain_scratch(n_row, n_col, rows_one, rows_two, depth, rank):
    n, chips, plane = n_row * n_col, n_row * n_col // 2, n_row // 2
    half, blocks, chunk, n_one, n_two = depth // 2, rank // chips, rank // plane, LANES, LANES
    share, portions, own_b = rank // n, half // LANES, rank // n_col

    def buffer(*shape):
        return pltpu.VMEM(shape, jnp.float32)

    def dma(*shape):
        return pltpu.SemaphoreType.DMA(shape)

    return dict(
        tensor=buffer(rows_one, rows_two, depth),
        start=buffer(rank, depth),
        part_one=buffer(rows_one, rank),
        part_two=buffer(rows_two, rank),
        parted=buffer(n * SUBLANES, LANES),
        held=buffer(n * SUBLANES, LANES),
        faces=buffer(share * n_one, n_two),
        turned=buffer(share, n_two, n_one),
        all_one=buffer(n_one, rank),
        all_two=buffer(n_two, rank),
        gram_part=buffer(2, LANES, LANES),
        gram_parts=buffer(2, n_row, LANES // n_row, LANES),
        gram_planes=buffer(2, n_col, LANES // n_row, LANES),
        gram_sum=buffer(2, LANES, LANES),
        basis_one=buffer(rank, n_one),
        basis_two=buffer(rank, n_two),
        factors=buffer(2, rank, LANES),
        block=buffer(portions, n_one, SUBLANES, LANES),
        mixed=buffer(portions, rank, SUBLANES, LANES),
        joined=buffer(portions, blocks, n_two, LANES),
        slab=buffer(blocks * rank, half),
        linv=buffer(rank, rank),
        image=buffer(STEPS + 1, portions, rank, LANES),
        cross_own=buffer(STEPS, rank, blocks * rank),
        cross_pair=buffer(STEPS, rank, blocks * rank),
        inner_own=buffer(STEPS + 1, rank, rank),
        inner_pair=buffer(STEPS + 1, rank, rank),
        image_part=buffer(STEPS, portions, rank, LANES),
        image_parts=buffer(STEPS, portions, plane, chunk, LANES),
        image_planes=buffer(STEPS, portions, n_col, chunk, LANES),
        last=buffer(2, rank, half),
        core_own=buffer(blocks * rank, rank),
        core_pair=buffer(blocks * rank, rank),
        core_sum=buffer(blocks, rank, rank),
        core_all=buffer(n_col * blocks, own_b, rank),
        loaded=dma(4),
        stored=dma(6),
        d_held=dma(2),
        d_one=dma(2),
        d_two=dma(2),
        d_block=dma(2),
        kept=dma(1),
        d_gram_row=dma(2, 2),
        d_gram_col=dma(2, 2),
        d_gram_all=dma(2, 2),
        d_mixed=dma(2),
        d_cross=dma(2, 2),
        d_inner=dma(2, 2),
        d_image_row=dma(portions, 2),
        d_image_col=dma(2, portions, 2),
        d_image_all=dma(portions, 2),
        d_last=dma(2),
        d_wide=dma(2),
        d_core=dma(2),
    )


def chain_kernel(n_row, n_col, names, *refs):
    ins, outs, refs = refs[:4], refs[4:9], refs[9:]
    g = types.SimpleNamespace(**dict(zip(names, refs)))
    t_ref, v_ref = g.tensor, g.start
    row, col = lax.axis_index("row"), lax.axis_index("col")
    n, plane, chips = n_row * n_col, n_row // 2, n_row * n_col // 2
    me, chip, core = row * n_col + col, row // 2, lax.rem(row, 2)
    other = row + 1 - 2 * core
    rows_one, rows_two, depth = t_ref.shape
    rank, half = v_ref.shape[0], depth // 2
    share, tiles, portions = rank // n, rows_one * rows_two // LANES, half // LANES
    n_one = n_two = LANES
    row_peers = [lax.rem(row + d, n_row) for d in range(n_row)]
    col_peers = [lax.rem(col + d, n_col) for d in range(n_col)]
    chip_peers = [lax.rem(chip + d, plane) for d in range(plane)]
    far = sorted(
        [(a, b) for a in range(n_row) for b in range(n_col) if a or b], key=lambda at: -min(at[1], n_col - at[1])
    )

    def pair(sems, k):
        return (sems.at[k, 0], sems.at[k, 1])

    def ends(sems):
        return (sems.at[0], sems.at[1])

    parts = (t_ref, v_ref, g.part_one, g.part_two)
    loads = [pltpu.make_async_copy(ins[k], parts[k], g.loaded.at[k]) for k in range(4)]
    start_all(loads)
    barrier = pltpu.get_barrier_semaphore()
    for a, b in far:
        pl.semaphore_signal(barrier, inc=1, device_id=(row_peers[a], col_peers[b]), device_id_type=MESH)
    for copy in loads:
        copy.wait()
    contracted = right_product(v_ref[...], t_ref[...].reshape(rows_one * rows_two, depth))
    for tile in range(tiles):
        g.parted[pl.ds(tile, rank, stride=tiles), :] = contracted[:, tile * LANES : (tile + 1) * LANES]
    pl.semaphore_wait(barrier, n - 1)
    place = aligned((col * n_row + row) * SUBLANES, SUBLANES)
    start_all(
        [
            remote(
                g.parted.at[aligned((row_peers[a] * n_col + col_peers[b]) * SUBLANES, SUBLANES), :],
                g.held.at[place, :], ends(g.d_held), row_peers[a], col_peers[b],
            )
            for a, b in far
        ]
    )
    own_one, own_two = aligned(row * rows_one, rows_one), aligned(col * rows_two, rows_two)
    start_all([remote(g.part_two, g.all_two.at[own_two, :], ends(g.d_two), row, col_peers[d]) for d in range(1, n_col)])
    start_all([remote(g.part_one, g.all_one.at[own_one, :], ends(g.d_one), row_peers[d], col) for d in range(1, n_row)])

    def block_source(which, peer):
        return t_ref.at[
            :,
            aligned(peer // 2 * SUBLANES, SUBLANES),
            aligned(lax.rem(peer, 2) * half + which * LANES, LANES, LANES),
        ]

    def block_target(which):
        return g.block.at[which, pl.ds(row * rows_one, rows_one)]

    def block_start(which):
        start_all(
            [
                remote(block_source(which, row_peers[d]), block_target(which), ends(g.d_block), row_peers[d], col)
                for d in range(1, n_row)
            ]
        )

    block_start(0)
    start_all([pltpu.make_async_copy(block_source(w, row), block_target(w), g.kept.at[0]) for w in range(portions)])
    g.held[place, :] = g.parted[aligned(me * SUBLANES, SUBLANES), :]
    g.all_one[own_one, :] = g.part_one[...]
    g.all_two[own_two, :] = g.part_two[...]
    for w in range(portions):
        g.image[0, w] = v_ref[:, aligned(core * half + w * LANES, LANES, LANES)]
    g.linv[...] = unit(rank)
    for end in range(2):
        wait_bytes(g.all_two.at[pl.ds(0, n_two - rows_two), :], g.d_two.at[end])
        wait_bytes(g.all_one.at[pl.ds(0, n_one - rows_one), :], g.d_one.at[end])
        wait_bytes(g.held.at[pl.ds(0, (n - 1) * SUBLANES), :], g.d_held.at[end])
    group = lane_groups(rows_two)
    for c in range(share):
        for tile in range(tiles):
            blocks = [
                g.held[pl.ds(q * n_row * SUBLANES + c * tiles + tile, n_row, stride=SUBLANES), :] for q in range(n_col)
            ]
            for s in range(n_col):
                line = shifted(blocks[0], -s * rows_two)
                for q in range(1, n_col):
                    line = jnp.where(group == q, shifted(blocks[q], (q - s) * rows_two), line)
                g.faces[pl.ds(c * n_one + tile * n_col + s, n_row, stride=rows_one), :] = line

    count = LANES // n_row
    own_rows = aligned(row * count, count)

    def gram_first(w):
        start_all(
            [
                remote(
                    g.gram_part.at[w, aligned(row_peers[d] * count, count), :], g.gram_parts.at[w, d],
                    pair(g.d_gram_row, w), row_peers[d], col,
                )
                for d in range(1, n_row)
            ]
        )

    def gram_second(w):
        wait_bytes(g.gram_parts.at[w, pl.ds(0, n_row - 1)], g.d_gram_row.at[w, 1])
        total = g.gram_part[w, own_rows, :]
        for d in range(1, n_row):
            total = total + g.gram_parts[w, d]
        g.gram_planes[w, col] = total
        start_all(
            [
                remote(g.gram_planes.at[w, col], g.gram_planes.at[w, col], pair(g.d_gram_col, w), row, col_peers[d])
                for d in range(1, n_col)
            ]
        )

    def gram_third(w):
        wait_bytes(g.gram_planes.at[w, pl.ds(0, n_col - 1)], g.d_gram_col.at[w, 1])
        total = g.gram_planes[w, 0]
        for q in range(1, n_col):
            total = total + g.gram_planes[w, q]
        g.gram_sum[w, own_rows, :] = total
        start_all(
            [
                remote(
                    g.gram_sum.at[w, own_rows, :], g.gram_sum.at[w, own_rows, :],
                    pair(g.d_gram_all, w), row_peers[d], col,
                )
                for d in range(1, n_row)
            ]
        )

    def gram_end(w):
        wait_bytes(g.gram_sum.at[w, pl.ds(0, LANES - count), :], g.d_gram_all.at[w, 1])
        wait_bytes(g.gram_parts.at[w, pl.ds(0, n_row - 1)], g.d_gram_row.at[w, 0])
        wait_bytes(g.gram_planes.at[w, pl.ds(0, n_col - 1)], g.d_gram_col.at[w, 0])
        wait_bytes(g.gram_sum.at[w, pl.ds(0, LANES - count), :], g.d_gram_all.at[w, 0])

    def self_gram(slabs):
        total = right_product(slabs[0], slabs[0])
        for slab in slabs[1:]:
            total = total + right_product(slab, slab)
        return total

    g.gram_part[0] = self_gram(
        [product(g.faces[c * n_one : (c + 1) * n_one, :], g.all_two[...]) for c in range(share)]
    )
    gram_first(0)
    for c in range(share):
        g.turned[c] = g.faces[c * n_one : (c + 1) * n_one, :].T
    g.basis_one[...] = g.all_one[...].T
    g.basis_two[...] = g.all_two[...].T
    gram_second(0)
    block_start(1)
    gram_third(0)
    gram_end(0)
    for which in range(2, portions):
        block_start(which)
    settle_turned(g.gram_sum.at[0], g.basis_one)
    basis_one = g.basis_one[...]

    g.gram_part[1] = self_gram([right_product(g.turned[c], basis_one) for c in range(share)])
    gram_first(1)
    g.factors[0] = basis_one * math.sqrt(n_one)
    for end in range(2):
        wait_bytes(g.block.at[:, pl.ds(0, n_one - rows_one)], g.d_block.at[end])
    wait_bytes(g.block.at[:, pl.ds(0, rows_one)], g.kept.at[0])
    flat_block = g.block.reshape(portions * n_one * SUBLANES, LANES)
    flat_mixed = g.mixed.reshape(portions * rank * SUBLANES, LANES)
    for s in range(SUBLANES):
        face = [flat_block[pl.ds(w * n_one * SUBLANES + s, n_one, stride=SUBLANES), :] for w in range(portions)]
        face = product(basis_one, jnp.concatenate(face, axis=1))
        for w in range(portions):
            flat_mixed[pl.ds(w * rank * SUBLANES + s, rank, stride=SUBLANES), :] = face[:, w * LANES : (w + 1) * LANES]
    gram_second(1)
    pieces = rank // chips
    place = chip * n_col + col
    lines = aligned(col * rows_two + chip * SUBLANES, SUBLANES)
    start_all(
        [
            remote(
                g.mixed.at[:, pl.ds((chip_peers[a] * n_col + col_peers[b]) * pieces, pieces)], g.joined.at[:, :, lines, :],
                ends(g.d_mixed), chip_peers[a] * 2 + core, col_peers[b],
            )
            for a, b in far
            if a < plane
        ]
    )
    gram_third(1)
    g.joined[:, :, lines, :] = g.mixed[:, pl.ds(place * pieces, pieces)]
    gram_end(1)
    settle_turned(g.gram_sum.at[1], g.basis_two)
    basis_two = g.basis_two[...]
    g.factors[1] = basis_two * math.sqrt(n_two)
    stores = [pltpu.make_async_copy(g.factors.at[k], outs[k], g.stored.at[k]) for k in range(2)]
    start_all(stores)
    for end in range(2):
        wait_bytes(g.mixed.at[:, pl.ds(0, rank - pieces)], g.d_mixed.at[end])
    for a in range(pieces):
        g.slab[a * rank : (a + 1) * rank, :] = product(
            basis_two, jnp.concatenate([g.joined[w, a] for w in range(portions)], axis=1)
        )

    chunk = rank // plane
    own_chunk = aligned(chip * chunk, chunk)

    def swap(source, target, sems):
        copy = remote(source, target, ends(sems), other, col)
        copy.start()
        return copy

    def lanes(value, w):
        return value[:, w * LANES : (w + 1) * LANES]

    def scaled(step, w):
        return product(g.linv[...], g.image[step, w])

    def one(step, carry):
        turn = lax.rem(step, 2)
        iterate, cross, inner = [], None, None
        for w in range(portions):
            @pl.when(step > 0)
            def _():
                wait_bytes(g.image.at[step, w, pl.ds(0, rank - chunk), :], g.d_image_all.at[w, 1])
                wait_bytes(g.image.at[step, w, pl.ds(0, rank - chunk), :], g.d_image_all.at[w, 0])

            now = scaled(step, w)
            iterate.append(now)
            term = right_product(now, g.slab[:, w * LANES : (w + 1) * LANES])
            cross = term if cross is None else cross + term
        g.cross_own[step] = cross
        crossing = swap(g.cross_own.at[step], g.cross_pair.at[step], g.d_cross.at[turn])
        for now in iterate:
            term = right_product(now, now)
            inner = term if inner is None else inner + term
        g.inner_own[step] = inner
        meeting = swap(g.inner_own.at[step], g.inner_pair.at[step], g.d_inner.at[turn])
        crossing.wait()
        cross = g.cross_own[step] + g.cross_pair[step]
        for w in range(portions):
            g.image_part[step, w] = product(cross, g.slab[:, w * LANES : (w + 1) * LANES])
            start_all(
                [
                    remote(
                        g.image_part.at[step, w, aligned(chip_peers[d] * chunk, chunk), :], g.image_parts.at[step, w, d],
                        pair(g.d_image_row, w), chip_peers[d] * 2 + core, col,
                    )
                    for d in range(1, plane)
                ]
            )
        meeting.wait()
        for w in range(portions):
            wait_bytes(g.image_parts.at[step, w, pl.ds(0, plane - 1)], g.d_image_row.at[w, 1])
            total = g.image_part[step, w, own_chunk, :]
            for d in range(1, plane):
                total = total + g.image_parts[step, w, d]
            g.image_planes[step, w, col] = total
            start_all(
                [
                    remote(
                        g.image_planes.at[step, w, col], g.image_planes.at[step, w, col],
                        pair(g.d_image_col.at[turn], w), row, col_peers[d],
                    )
                    for d in range(1, n_col)
                ]
            )
        inverse = inverse_factor(g.inner_own[step] + g.inner_pair[step])
        g.linv[...] = jnp.where(step == 0, unit(rank), inverse)
        for w in range(portions):
            wait_bytes(g.image_planes.at[step, w, pl.ds(0, n_col - 1)], g.d_image_col.at[turn, w, 1])
            total = g.image_planes[step, w, 0]
            for q in range(1, n_col):
                total = total + g.image_planes[step, w, q]
            g.image[step + 1, w, own_chunk, :] = total
            start_all(
                [
                    remote(
                        g.image.at[step + 1, w, own_chunk, :], g.image.at[step + 1, w, own_chunk, :],
                        pair(g.d_image_all, w), chip_peers[d] * 2 + core, col,
                    )
                    for d in range(1, plane)
                ]
            )
        for w in range(portions):
            wait_bytes(g.image_parts.at[step, w, pl.ds(0, plane - 1)], g.d_image_row.at[w, 0])
            wait_bytes(g.image_planes.at[step, w, pl.ds(0, n_col - 1)], g.d_image_col.at[turn, w, 0])
        return carry

    lax.fori_loop(0, STEPS, one, 0)
    inner, cross = None, None
    for w in range(portions):
        for end in (1, 0):
            wait_bytes(g.image.at[STEPS, w, pl.ds(0, rank - chunk), :], g.d_image_all.at[w, end])
        now = scaled(STEPS, w)
        g.last[0, :, w * LANES : (w + 1) * LANES] = now
        term = right_product(g.slab[:, w * LANES : (w + 1) * LANES], now)
        cross = term if cross is None else cross + term
    g.core_own[...] = cross
    crossing = swap(g.core_own, g.core_pair, g.d_last)
    for w in range(portions):
        now = g.last[0, :, w * LANES : (w + 1) * LANES]
        term = right_product(now, now)
        inner = term if inner is None else inner + term
    g.inner_own[STEPS] = inner
    meeting = swap(g.inner_own.at[STEPS], g.inner_pair.at[STEPS], g.d_inner.at[STEPS % 2])
    lasting = swap(g.last.at[0], g.last.at[1], g.d_wide)
    crossing.wait()
    g.core_sum[...] = (g.core_own[...] + g.core_pair[...]).reshape(pieces, rank, rank)
    own_b = rank // n_col
    own_pieces = pl.ds(col * pieces, pieces)
    start_all(
        [
            remote(
                g.core_sum.at[:, aligned(col_peers[d] * own_b, own_b), :], g.core_all.at[own_pieces],
                ends(g.d_core), row, col_peers[d],
            )
            for d in range(1, n_col)
        ]
    )
    g.core_all[own_pieces] = g.core_sum[:, aligned(col * own_b, own_b), :]
    meeting.wait()
    lasting.wait()
    for k, owner in enumerate((core, 1 - core)):
        stores.append(
            pltpu.make_async_copy(
                g.last.at[k], outs[2].at[:, aligned(owner * half, half, LANES)], g.stored.at[2 + k]
            )
        )
        stores[-1].start()
    g.linv[...] = inverse_factor(g.inner_own[STEPS] + g.inner_pair[STEPS])
    stores.append(pltpu.make_async_copy(g.linv, outs[3], g.stored.at[4]))
    stores[-1].start()
    for end in (1, 0):
        wait_bytes(g.core_all.at[pl.ds(0, (n_col - 1) * pieces)], g.d_core.at[end])
    own_a = outs[4].shape[0]
    stores.append(pltpu.make_async_copy(g.core_all.at[pl.ds(core * own_a, own_a)], outs[4], g.stored.at[5]))
    stores[-1].start()
    for copy in stores:
        copy.wait()


def finish_kernel(one_ref, two_ref, last_ref, linv_ref, piece_ref, f1_ref, f2_ref, f3_ref, core_ref):
    f1_ref[...] = one_ref[...]
    f2_ref[...] = two_ref[...]
    linv = linv_ref[...]
    f3_ref[...] = product(linv, last_ref[...]) * math.sqrt(last_ref.shape[1])
    core_ref[...] = right_product(piece_ref[...].reshape(core_ref.shape), linv)


def unit(size):
    shape = (size, size)
    return (lax.broadcasted_iota(jnp.int32, shape, 0) == lax.broadcasted_iota(jnp.int32, shape, 1)).astype(jnp.float32)


def shared(n_row, n_col, tensor, start_one, start_two, start_three):
    rows_one, rows_two, depth = tensor.shape
    rank = start_three.shape[1]
    own_a, own_b = rank // n_row, rank // n_col
    spec = pl.BlockSpec(memory_space=pltpu.VMEM)
    scratch = chain_scratch(n_row, n_col, rows_one, rows_two, depth, rank)

    def outs(*shapes):
        return [jax.ShapeDtypeStruct(shape, jnp.float32) for shape in shapes]

    chained = pl.pallas_call(
        functools.partial(chain_kernel, n_row, n_col, tuple(scratch)),
        out_shape=outs((rank, LANES), (rank, LANES), (rank, depth), (rank, rank), (own_a, own_b, rank)),
        in_specs=[pl.BlockSpec(memory_space=pltpu.HBM)] * 4,
        out_specs=[pl.BlockSpec(memory_space=pltpu.HBM)] * 5,
        scratch_shapes=list(scratch.values()),
        compiler_params=pltpu.CompilerParams(
            collective_id=1, has_side_effects=True, vmem_limit_bytes=67043328 - 300 * 1024
        ),
        cost_estimate=pl.CostEstimate(flops=10**9, bytes_accessed=10**7, transcendentals=0),
        name="chain",
    )(tensor, start_three.T, start_one, start_two)
    factor_one, factor_two, factor_three, core = pl.pallas_call(
        finish_kernel,
        out_shape=outs((rank, LANES), (rank, LANES), (rank, depth), (own_a * own_b, rank)),
        in_specs=[spec] * 5,
        out_specs=[spec] * 4,
        compiler_params=pltpu.CompilerParams(vmem_limit_bytes=67043328 - 100 * 1024),
        cost_estimate=pl.CostEstimate(flops=10**7, bytes_accessed=10**6, transcendentals=0),
        name="finish",
    )(*chained)
    return (factor_one.T, factor_two.T, factor_three.T, core.reshape(own_a, own_b, rank).transpose(2, 0, 1))


def solution(mesh):
    n_row, n_col = mesh.shape["row"], mesh.shape["col"]
    n = n_row * n_col

    def on_device(tensor, start_one, start_two, start_three):
        rows_one, rows_two, depth = tensor.shape
        rank = start_three.shape[1]
        plane, span = n_row // 2, rows_one * rows_two
        even = (
            n_row % 2 == 0
            and rows_one * n_row == rows_two * n_col == LANES
            and rows_two == plane * SUBLANES
            and rows_one % SUBLANES == 0
            and depth % (2 * LANES) == 0
            and rank % (plane * SUBLANES) == 0
            and rank % (n_col * SUBLANES) == 0
            and rank % n == 0
            and rank // n * (span // LANES) == SUBLANES
        )
        if even:
            return shared(n_row, n_col, tensor, start_one, start_two, start_three)
        return general(tensor, start_one, start_two, start_three)

    return jax.shard_map(
        on_device,
        mesh=mesh,
        in_specs=(P("row", "col", None), P("row", None), P("col", None), P()),
        out_specs=(P(), P(), P(), P(None, "row", "col")),
        check_vma=False,
    )
```

time: 138 us -> 120 us (0.87)
  Pallas kernels: 130 us -> 119 us
  local copies, waits for them, and re-layouts: 6.85 us -> 0 us
    pallas_call x1, Pallas kernels: 128 us -> 117 us  [shared(): pl.pallas_call(functools.partial(chain_kernel, n_row, n_col, tuple(scratc...]
    unnamed x18 -> x0, local copies, waits for them, and re-layouts: 6.85 us -> none
where the time goes in v2:
time: 120 us
  Pallas kernels  119 us (99%)
    pallas_call x1, Pallas kernels, shared(): pl.pallas_call(functools.partial(chain_kernel, n_row, n_col, tuple(scratc...  117 us

profile of v2, /device:TPU:0, one launch (start us, length us, event | category | flops | bytes accessed | tf_op | source)
XLA Modules:
  0.0 119.6 jit_solution(18305084393792991651)
XLA Ops:
  0.6 116.9 %chain.1 = (f32[64,128]{1,0:T(8,128)}, f32[64,128]{1,0:T(8,128)}, f32[64,768]{1,0:T(8,128)}, f32[64,64]{1,0:T(8,128)}, f32[8,16,64]{2,1,0:T(8,128)}) custom-call(f32[16,32,768]{2,1,0:T(8,128)} %refs_0_.1, f32[64,768]{1,0:T(8,128)} %bitcast.7, f32[16,64]{1,0:T(8,128)} %refs_2_.1, f32[32,64]{1,0:T(8,128)} %refs_3_.1), custom_call_target="tpu_custom_call" | custom-call | flops 1000000000 | bytes 10000000 | tf_op jit(solution)/shard_map/chain/pallas_call | solution.py:623
  117.5 2.1 %finish.1 = (f32[64,128]{1,0:T(8,128)}, f32[64,128]{1,0:T(8,128)}, f32[64,768]{1,0:T(8,128)}, f32[128,64]{1,0:T(8,128)}) custom-call(f32[64,128]{1,0:T(8,128)} %get-tuple-element.13.one_ref, f32[64,128]{1,0:T(8,128)} %get-tuple-element.14.two_ref, f32[64,768]{1,0:T(8,128)} %get-tuple-element.15.last_ref, f32[64,64]{1,0:T(8,128)} %get-tuple-element.16.linv_ref, ...), custom_call_target="tpu_custom_call" | custom-call | flops 10000000 | bytes 1000000 | tf_op jit(solution)/shard_map/finish/pallas_call | solution.py:635

commit v3 on v2

--- a/solution.py
+++ b/solution.py
@@ -16,6 +16,7 @@
 MESH = pl.DeviceIdType.MESH
 SUBLANES = 8
 LANES = 128
+BAND = 2 * LANES
 
 
 def product(left, right):
@@ -100,44 +101,55 @@
     return (factor_one, factor_two, factor_three, core)
 
 
+def unit(size):
+    shape = (size, size)
+    return (lax.broadcasted_iota(jnp.int32, shape, 0) == lax.broadcasted_iota(jnp.int32, shape, 1)).astype(jnp.float32)
+
+
 def inverse_factor(inner):
     n = inner.shape[0]
     groups = n // SUBLANES
-    eye = (
-        lax.broadcasted_iota(jnp.int32, (n, n), 0) == lax.broadcasted_iota(jnp.int32, (n, n), 1)
-    ).astype(jnp.float32)
-    whole = jnp.concatenate([inner, eye], axis=1)
-    width = whole.shape[1]
+    whole = jnp.concatenate([inner, unit(n)], axis=1)
+    shape = (SUBLANES, whole.shape[1])
     rows = [whole[g * SUBLANES : (g + 1) * SUBLANES] for g in range(groups)]
-    sub = lax.broadcasted_iota(jnp.int32, (SUBLANES, width), 0)
-    pivots = [None] * n
-    shape = (SUBLANES, width)
+    sub = lax.broadcasted_iota(jnp.int32, shape, 0)
+    zero = rows[0] * 0.0
+
+    def across(value, t):
+        return jnp.broadcast_to(value[t : t + 1, :], shape)
+
+    def column(g, k):
+        return jnp.broadcast_to(rows[g][:, k : k + 1], shape)
+
+    diagonal = [column(0, k) + zero for k in range(SUBLANES)]
+    out = []
     for base in range(groups):
-        columns = [
-            [jnp.broadcast_to(rows[g][:, k : k + 1], shape) for g in range(base, groups)]
-            for k in range(base * SUBLANES, (base + 1) * SUBLANES)
-        ]
+        head = base * SUBLANES
+        panel = [[column(g, head + k) for g in range(base + 1, groups)] for k in range(SUBLANES)]
+        coming = []
+        if base + 1 < groups:
+            coming = [column(base + 1, head + SUBLANES + k) for k in range(SUBLANES)]
+            panel[0][0] = panel[0][0] + zero
+        held = None
         for t in range(SUBLANES):
-            pivot = jnp.broadcast_to(columns[t][0][t : t + 1, :], shape)
+            pivot = across(diagonal[t], t)
+            held = pivot if held is None else jnp.where(sub >= t, pivot, held)
             scale = 1.0 / pivot
-            pivots[base * SUBLANES + t] = pivot
-            row = jnp.broadcast_to(rows[base][t : t + 1, :], shape)
-            heads = [
-                jnp.broadcast_to(columns[s][0][t : t + 1, :], shape) for s in range(t + 1, SUBLANES)
-            ]
-            for g in range(base, groups):
-                factor = columns[t][g - base] * scale
-                if g == base:
-                    factor = jnp.where(sub > t, factor, 0.0)
+            row = across(rows[base], t)
+            heads = [across(diagonal[s], t) for s in range(t + 1, SUBLANES)]
+            factor = jnp.where(sub > t, diagonal[t] * scale, 0.0)
+            for s in range(t + 1, SUBLANES):
+                diagonal[s] = diagonal[s] - factor * heads[s - t - 1]
+            rows[base] = rows[base] - factor * row
+            for k, g in enumerate(range(base + 1, groups)):
+                factor = panel[t][k] * scale
+                if k == 0:
+                    coming = [coming[s] - factor * across(panel[t][0], s) for s in range(SUBLANES)]
                 rows[g] = rows[g] - factor * row
                 for s in range(t + 1, SUBLANES):
-                    columns[s][g - base] = columns[s][g - base] - factor * heads[s - t - 1]
-    out = []
-    for g in range(groups):
-        held = pivots[g * SUBLANES]
-        for t in range(1, SUBLANES):
-            held = jnp.where(sub == t, pivots[g * SUBLANES + t], held)
-        out.append(rows[g] * lax.rsqrt(held))
+                    panel[s][k] = panel[s][k] - factor * heads[s - t - 1]
+        out.append(rows[base] * lax.rsqrt(held))
+        diagonal = coming
     return jnp.concatenate(out, axis=0)[:, n:]
 
 
@@ -184,9 +196,9 @@
 
 
 def chain_scratch(n_row, n_col, rows_one, rows_two, depth, rank):
-    n, chips, plane = n_row * n_col, n_row * n_col // 2, n_row // 2
-    half, blocks, chunk, n_one, n_two = depth // 2, rank // chips, rank // plane, LANES, LANES
-    share, portions, own_b = rank // n, half // LANES, rank // n_col
+    n, half, n_one, n_two = n_row * n_col, depth // 2, LANES, LANES
+    share, portions, pieces = rank // n, half // LANES, rank // n
+    bands, chunk, own_b = depth // BAND, rank // n_row, rank // n_col
 
     def buffer(*shape):
         return pltpu.VMEM(shape, jnp.float32)
@@ -214,24 +226,19 @@
         factors=buffer(2, rank, LANES),
         block=buffer(portions, n_one, SUBLANES, LANES),
         mixed=buffer(portions, rank, SUBLANES, LANES),
-        joined=buffer(portions, blocks, n_two, LANES),
-        slab=buffer(blocks * rank, half),
+        joined=buffer(2 * portions, pieces, n_two, LANES),
+        slab=buffer(pieces * rank, depth),
         linv=buffer(rank, rank),
-        image=buffer(STEPS + 1, portions, rank, LANES),
-        cross_own=buffer(STEPS, rank, blocks * rank),
-        cross_pair=buffer(STEPS, rank, blocks * rank),
-        inner_own=buffer(STEPS + 1, rank, rank),
-        inner_pair=buffer(STEPS + 1, rank, rank),
-        image_part=buffer(STEPS, portions, rank, LANES),
-        image_parts=buffer(STEPS, portions, plane, chunk, LANES),
-        image_planes=buffer(STEPS, portions, n_col, chunk, LANES),
-        last=buffer(2, rank, half),
-        core_own=buffer(blocks * rank, rank),
-        core_pair=buffer(blocks * rank, rank),
-        core_sum=buffer(blocks, rank, rank),
-        core_all=buffer(n_col * blocks, own_b, rank),
+        iterate=buffer(rank, depth),
+        cross=buffer(rank, pieces * rank),
+        image=buffer(STEPS, bands, rank, BAND),
+        image_part=buffer(STEPS, bands, rank, BAND),
+        image_parts=buffer(STEPS, bands, n_row, chunk, BAND),
+        image_planes=buffer(STEPS, bands, n_col, chunk, BAND),
+        core_own=buffer(pieces, rank, rank),
+        core_all=buffer(n_col * pieces, own_b, rank),
         loaded=dma(4),
-        stored=dma(6),
+        stored=dma(5),
         d_held=dma(2),
         d_one=dma(2),
         d_two=dma(2),
@@ -241,13 +248,9 @@
         d_gram_col=dma(2, 2),
         d_gram_all=dma(2, 2),
         d_mixed=dma(2),
-        d_cross=dma(2, 2),
-        d_inner=dma(2, 2),
-        d_image_row=dma(portions, 2),
-        d_image_col=dma(2, portions, 2),
-        d_image_all=dma(portions, 2),
-        d_last=dma(2),
-        d_wide=dma(2),
+        d_image_row=dma(bands, 2),
+        d_image_col=dma(2, bands, 2),
+        d_image_all=dma(bands, 2),
         d_core=dma(2),
     )
 
@@ -257,16 +260,14 @@
     g = types.SimpleNamespace(**dict(zip(names, refs)))
     t_ref, v_ref = g.tensor, g.start
     row, col = lax.axis_index("row"), lax.axis_index("col")
-    n, plane, chips = n_row * n_col, n_row // 2, n_row * n_col // 2
+    n = n_row * n_col
     me, chip, core = row * n_col + col, row // 2, lax.rem(row, 2)
-    other = row + 1 - 2 * core
     rows_one, rows_two, depth = t_ref.shape
     rank, half = v_ref.shape[0], depth // 2
     share, tiles, portions = rank // n, rows_one * rows_two // LANES, half // LANES
     n_one = n_two = LANES
     row_peers = [lax.rem(row + d, n_row) for d in range(n_row)]
     col_peers = [lax.rem(col + d, n_col) for d in range(n_col)]
-    chip_peers = [lax.rem(chip + d, plane) for d in range(plane)]
     far = sorted(
         [(a, b) for a in range(n_row) for b in range(n_col) if a or b], key=lambda at: -min(at[1], n_col - at[1])
     )
@@ -326,9 +327,6 @@
     g.held[place, :] = g.parted[aligned(me * SUBLANES, SUBLANES), :]
     g.all_one[own_one, :] = g.part_one[...]
     g.all_two[own_two, :] = g.part_two[...]
-    for w in range(portions):
-        g.image[0, w] = v_ref[:, aligned(core * half + w * LANES, LANES, LANES)]
-    g.linv[...] = unit(rank)
     for end in range(2):
         wait_bytes(g.all_two.at[pl.ds(0, n_two - rows_two), :], g.d_two.at[end])
         wait_bytes(g.all_one.at[pl.ds(0, n_one - rows_one), :], g.d_one.at[end])
@@ -431,21 +429,20 @@
         for w in range(portions):
             flat_mixed[pl.ds(w * rank * SUBLANES + s, rank, stride=SUBLANES), :] = face[:, w * LANES : (w + 1) * LANES]
     gram_second(1)
-    pieces = rank // chips
-    place = chip * n_col + col
+    pieces = rank // n
     lines = aligned(col * rows_two + chip * SUBLANES, SUBLANES)
+    parts = pl.ds(core * portions, portions)
     start_all(
         [
             remote(
-                g.mixed.at[:, pl.ds((chip_peers[a] * n_col + col_peers[b]) * pieces, pieces)], g.joined.at[:, :, lines, :],
-                ends(g.d_mixed), chip_peers[a] * 2 + core, col_peers[b],
+                g.mixed.at[:, pl.ds((row_peers[a] * n_col + col_peers[b]) * pieces, pieces)], g.joined.at[parts, :, lines, :],
+                ends(g.d_mixed), row_peers[a], col_peers[b],
             )
             for a, b in far
-            if a < plane
         ]
     )
     gram_third(1)
-    g.joined[:, :, lines, :] = g.mixed[:, pl.ds(place * pieces, pieces)]
+    g.joined[parts, :, lines, :] = g.mixed[:, pl.ds(me * pieces, pieces)]
     gram_end(1)
     settle_turned(g.gram_sum.at[1], g.basis_two)
     basis_two = g.basis_two[...]
@@ -456,63 +453,44 @@
         wait_bytes(g.mixed.at[:, pl.ds(0, rank - pieces)], g.d_mixed.at[end])
     for a in range(pieces):
         g.slab[a * rank : (a + 1) * rank, :] = product(
-            basis_two, jnp.concatenate([g.joined[w, a] for w in range(portions)], axis=1)
+            basis_two, jnp.concatenate([g.joined[w, a] for w in range(2 * portions)], axis=1)
         )
 
-    chunk = rank // plane
-    own_chunk = aligned(chip * chunk, chunk)
-
-    def swap(source, target, sems):
-        copy = remote(source, target, ends(sems), other, col)
-        copy.start()
-        return copy
-
-    def lanes(value, w):
-        return value[:, w * LANES : (w + 1) * LANES]
-
-    def scaled(step, w):
-        return product(g.linv[...], g.image[step, w])
+    bands, chunk = depth // BAND, rank // n_row
+    own_chunk = aligned(row * chunk, chunk)
+
+    def band(ref, w):
+        return ref[:, w * BAND : (w + 1) * BAND]
+
+    def added(terms):
+        total = terms[0]
+        for term in terms[1:]:
+            total = total + term
+        return total
+
+    def inner():
+        return added([right_product(band(g.iterate, w), band(g.iterate, w)) for w in range(bands)])
 
     def one(step, carry):
         turn = lax.rem(step, 2)
-        iterate, cross, inner = [], None, None
-        for w in range(portions):
-            @pl.when(step > 0)
-            def _():
-                wait_bytes(g.image.at[step, w, pl.ds(0, rank - chunk), :], g.d_image_all.at[w, 1])
-                wait_bytes(g.image.at[step, w, pl.ds(0, rank - chunk), :], g.d_image_all.at[w, 0])
-
-            now = scaled(step, w)
-            iterate.append(now)
-            term = right_product(now, g.slab[:, w * LANES : (w + 1) * LANES])
-            cross = term if cross is None else cross + term
-        g.cross_own[step] = cross
-        crossing = swap(g.cross_own.at[step], g.cross_pair.at[step], g.d_cross.at[turn])
-        for now in iterate:
-            term = right_product(now, now)
-            inner = term if inner is None else inner + term
-        g.inner_own[step] = inner
-        meeting = swap(g.inner_own.at[step], g.inner_pair.at[step], g.d_inner.at[turn])
-        crossing.wait()
-        cross = g.cross_own[step] + g.cross_pair[step]
-        for w in range(portions):
-            g.image_part[step, w] = product(cross, g.slab[:, w * LANES : (w + 1) * LANES])
+        cross = g.cross[...]
+        for w in range(bands):
+            g.image_part[step, w] = product(cross, band(g.slab, w))
             start_all(
                 [
                     remote(
-                        g.image_part.at[step, w, aligned(chip_peers[d] * chunk, chunk), :], g.image_parts.at[step, w, d],
-                        pair(g.d_image_row, w), chip_peers[d] * 2 + core, col,
+                        g.image_part.at[step, w, aligned(row_peers[d] * chunk, chunk), :], g.image_parts.at[step, w, d],
+                        pair(g.d_image_row, w), row_peers[d], col,
                     )
-                    for d in range(1, plane)
+                    for d in range(1, n_row)
                 ]
             )
-        meeting.wait()
-        for w in range(portions):
-            wait_bytes(g.image_parts.at[step, w, pl.ds(0, plane - 1)], g.d_image_row.at[w, 1])
-            total = g.image_part[step, w, own_chunk, :]
-            for d in range(1, plane):
-                total = total + g.image_parts[step, w, d]
-            g.image_planes[step, w, col] = total
+        square = inner()
+        for w in range(bands):
+            wait_bytes(g.image_parts.at[step, w, pl.ds(0, n_row - 1)], g.d_image_row.at[w, 1])
+            g.image_planes[step, w, col] = added(
+                [g.image_part[step, w, own_chunk, :]] + [g.image_parts[step, w, d] for d in range(1, n_row)]
+            )
             start_all(
                 [
                     remote(
@@ -522,76 +500,57 @@
                     for d in range(1, n_col)
                 ]
             )
-        inverse = inverse_factor(g.inner_own[step] + g.inner_pair[step])
-        g.linv[...] = jnp.where(step == 0, unit(rank), inverse)
-        for w in range(portions):
+        inverse = jnp.where(step == 0, unit(rank), inverse_factor(square))
+        g.linv[...] = inverse
+        for w in range(bands):
             wait_bytes(g.image_planes.at[step, w, pl.ds(0, n_col - 1)], g.d_image_col.at[turn, w, 1])
-            total = g.image_planes[step, w, 0]
-            for q in range(1, n_col):
-                total = total + g.image_planes[step, w, q]
-            g.image[step + 1, w, own_chunk, :] = total
+            g.image[step, w, own_chunk, :] = added([g.image_planes[step, w, q] for q in range(n_col)])
             start_all(
                 [
                     remote(
-                        g.image.at[step + 1, w, own_chunk, :], g.image.at[step + 1, w, own_chunk, :],
-                        pair(g.d_image_all, w), chip_peers[d] * 2 + core, col,
+                        g.image.at[step, w, own_chunk, :], g.image.at[step, w, own_chunk, :],
+                        pair(g.d_image_all, w), row_peers[d], col,
                     )
-                    for d in range(1, plane)
+                    for d in range(1, n_row)
                 ]
             )
-        for w in range(portions):
-            wait_bytes(g.image_parts.at[step, w, pl.ds(0, plane - 1)], g.d_image_row.at[w, 0])
+        terms = []
+        for w in range(bands):
+            wait_bytes(g.image.at[step, w, pl.ds(0, rank - chunk), :], g.d_image_all.at[w, 1])
+            now = product(g.linv[...], g.image[step, w])
+            g.iterate[:, w * BAND : (w + 1) * BAND] = now
+            terms.append(right_product(now, band(g.slab, w)))
+        g.cross[...] = added(terms)
+        for w in range(bands):
+            wait_bytes(g.image_parts.at[step, w, pl.ds(0, n_row - 1)], g.d_image_row.at[w, 0])
             wait_bytes(g.image_planes.at[step, w, pl.ds(0, n_col - 1)], g.d_image_col.at[turn, w, 0])
+            wait_bytes(g.image.at[step, w, pl.ds(0, rank - chunk), :], g.d_image_all.at[w, 0])
         return carry
 
+    g.iterate[...] = v_ref[...]
+    g.cross[...] = added([right_product(band(g.iterate, w), band(g.slab, w)) for w in range(bands)])
     lax.fori_loop(0, STEPS, one, 0)
-    inner, cross = None, None
-    for w in range(portions):
-        for end in (1, 0):
-            wait_bytes(g.image.at[STEPS, w, pl.ds(0, rank - chunk), :], g.d_image_all.at[w, end])
-        now = scaled(STEPS, w)
-        g.last[0, :, w * LANES : (w + 1) * LANES] = now
-        term = right_product(g.slab[:, w * LANES : (w + 1) * LANES], now)
-        cross = term if cross is None else cross + term
-    g.core_own[...] = cross
-    crossing = swap(g.core_own, g.core_pair, g.d_last)
-    for w in range(portions):
-        now = g.last[0, :, w * LANES : (w + 1) * LANES]
-        term = right_product(now, now)
-        inner = term if inner is None else inner + term
-    g.inner_own[STEPS] = inner
-    meeting = swap(g.inner_own.at[STEPS], g.inner_pair.at[STEPS], g.d_inner.at[STEPS % 2])
-    lasting = swap(g.last.at[0], g.last.at[1], g.d_wide)
-    crossing.wait()
-    g.core_sum[...] = (g.core_own[...] + g.core_pair[...]).reshape(pieces, rank, rank)
+    g.core_own[...] = g.cross[...].T.reshape(pieces, rank, rank)
     own_b = rank // n_col
     own_pieces = pl.ds(col * pieces, pieces)
     start_all(
         [
             remote(
-                g.core_sum.at[:, aligned(col_peers[d] * own_b, own_b), :], g.core_all.at[own_pieces],
+                g.core_own.at[:, aligned(col_peers[d] * own_b, own_b), :], g.core_all.at[own_pieces],
                 ends(g.d_core), row, col_peers[d],
             )
             for d in range(1, n_col)
         ]
     )
-    g.core_all[own_pieces] = g.core_sum[:, aligned(col * own_b, own_b), :]
-    meeting.wait()
-    lasting.wait()
-    for k, owner in enumerate((core, 1 - core)):
-        stores.append(
-            pltpu.make_async_copy(
-                g.last.at[k], outs[2].at[:, aligned(owner * half, half, LANES)], g.stored.at[2 + k]
-            )
-        )
-        stores[-1].start()
-    g.linv[...] = inverse_factor(g.inner_own[STEPS] + g.inner_pair[STEPS])
-    stores.append(pltpu.make_async_copy(g.linv, outs[3], g.stored.at[4]))
+    stores.append(pltpu.make_async_copy(g.iterate, outs[2], g.stored.at[2]))
+    stores[-1].start()
+    g.core_all[own_pieces] = g.core_own[:, aligned(col * own_b, own_b), :]
+    g.linv[...] = inverse_factor(inner())
+    stores.append(pltpu.make_async_copy(g.linv, outs[3], g.stored.at[3]))
     stores[-1].start()
     for end in (1, 0):
         wait_bytes(g.core_all.at[pl.ds(0, (n_col - 1) * pieces)], g.d_core.at[end])
-    own_a = outs[4].shape[0]
-    stores.append(pltpu.make_async_copy(g.core_all.at[pl.ds(core * own_a, own_a)], outs[4], g.stored.at[5]))
+    stores.append(pltpu.make_async_copy(g.core_all, outs[4], g.stored.at[4]))
     stores[-1].start()
     for copy in stores:
         copy.wait()
@@ -603,11 +562,6 @@
     linv = linv_ref[...]
     f3_ref[...] = product(linv, last_ref[...]) * math.sqrt(last_ref.shape[1])
     core_ref[...] = right_product(piece_ref[...].reshape(core_ref.shape), linv)
-
-
-def unit(size):
-    shape = (size, size)
-    return (lax.broadcasted_iota(jnp.int32, shape, 0) == lax.broadcasted_iota(jnp.int32, shape, 1)).astype(jnp.float32)
 
 
 def shared(n_row, n_col, tensor, start_one, start_two, start_three):
@@ -657,8 +611,8 @@
             and rows_one * n_row == rows_two * n_col == LANES
             and rows_two == plane * SUBLANES
             and rows_one % SUBLANES == 0
-            and depth % (2 * LANES) == 0
-            and rank % (plane * SUBLANES) == 0
+            and depth % BAND == 0
+            and rank % (n_row * SUBLANES) == 0
             and rank % (n_col * SUBLANES) == 0
             and rank % n == 0
             and rank // n * (span // LANES) == SUBLANES

time: 120 us -> 116 us (0.967)
  Pallas kernels: 119 us -> 115 us
    pallas_call x1, Pallas kernels: 117 us -> 113 us  [shared(): pl.pallas_call(functools.partial(chain_kernel, n_row, n_col, tuple(scratc...]
where the time goes in v3:
time: 116 us
  Pallas kernels  115 us (99%)
    pallas_call x1, Pallas kernels, shared(): pl.pallas_call(functools.partial(chain_kernel, n_row, n_col, tuple(scratc...  113 us

profile of v3, /device:TPU:0, one launch (start us, length us, event | category | flops | bytes accessed | tf_op | source)
XLA Modules:
  0.0 115.7 jit_solution(15025750089036331414)
XLA Ops:
  0.6 113.0 %chain.1 = (f32[64,128]{1,0:T(8,128)}, f32[64,128]{1,0:T(8,128)}, f32[64,768]{1,0:T(8,128)}, f32[64,64]{1,0:T(8,128)}, f32[8,16,64]{2,1,0:T(8,128)}) custom-call(f32[16,32,768]{2,1,0:T(8,128)} %refs_0_.1, f32[64,768]{1,0:T(8,128)} %bitcast.7, f32[16,64]{1,0:T(8,128)} %refs_2_.1, f32[32,64]{1,0:T(8,128)} %refs_3_.1), custom_call_target="tpu_custom_call" | custom-call | flops 1000000000 | bytes 10000000 | tf_op jit(solution)/shard_map/chain/pallas_call | solution.py:577
  113.6 2.1 %finish.1 = (f32[64,128]{1,0:T(8,128)}, f32[64,128]{1,0:T(8,128)}, f32[64,768]{1,0:T(8,128)}, f32[128,64]{1,0:T(8,128)}) custom-call(f32[64,128]{1,0:T(8,128)} %get-tuple-element.13.one_ref, f32[64,128]{1,0:T(8,128)} %get-tuple-element.14.two_ref, f32[64,768]{1,0:T(8,128)} %get-tuple-element.15.last_ref, f32[64,64]{1,0:T(8,128)} %get-tuple-element.16.linv_ref, ...), custom_call_target="tpu_custom_call" | custom-call | flops 10000000 | bytes 1000000 | tf_op jit(solution)/shard_map/finish/pallas_call | solution.py:589

commit v4 on v3

--- a/solution.py
+++ b/solution.py
@@ -227,15 +227,16 @@
         block=buffer(portions, n_one, SUBLANES, LANES),
         mixed=buffer(portions, rank, SUBLANES, LANES),
         joined=buffer(2 * portions, pieces, n_two, LANES),
-        slab=buffer(pieces * rank, depth),
+        slab=buffer(pieces, rank, depth),
+        core_slab=buffer(n_col * pieces, own_b, depth),
+        square=buffer(rank, rank),
         linv=buffer(rank, rank),
         iterate=buffer(rank, depth),
         cross=buffer(rank, pieces * rank),
-        image=buffer(STEPS, bands, rank, BAND),
+        image=buffer(STEPS + 1, bands, rank, BAND),
         image_part=buffer(STEPS, bands, rank, BAND),
         image_parts=buffer(STEPS, bands, n_row, chunk, BAND),
         image_planes=buffer(STEPS, bands, n_col, chunk, BAND),
-        core_own=buffer(pieces, rank, rank),
         core_all=buffer(n_col * pieces, own_b, rank),
         loaded=dma(4),
         stored=dma(5),
@@ -314,15 +315,16 @@
     def block_target(which):
         return g.block.at[which, pl.ds(row * rows_one, rows_one)]
 
-    def block_start(which):
+    def block_start(which, peers):
         start_all(
             [
                 remote(block_source(which, row_peers[d]), block_target(which), ends(g.d_block), row_peers[d], col)
-                for d in range(1, n_row)
+                for d in peers
             ]
         )
 
-    block_start(0)
+    middle = n_row // 2
+    block_start(0, range(1, n_row))
     start_all([pltpu.make_async_copy(block_source(w, row), block_target(w), g.kept.at[0]) for w in range(portions)])
     g.held[place, :] = g.parted[aligned(me * SUBLANES, SUBLANES), :]
     g.all_one[own_one, :] = g.part_one[...]
@@ -402,16 +404,17 @@
         [product(g.faces[c * n_one : (c + 1) * n_one, :], g.all_two[...]) for c in range(share)]
     )
     gram_first(0)
+    block_start(1, range(1, middle))
     for c in range(share):
         g.turned[c] = g.faces[c * n_one : (c + 1) * n_one, :].T
     g.basis_one[...] = g.all_one[...].T
     g.basis_two[...] = g.all_two[...].T
     gram_second(0)
-    block_start(1)
+    block_start(1, range(middle, n_row))
     gram_third(0)
+    for which in range(2, portions):
+        block_start(which, range(1, n_row))
     gram_end(0)
-    for which in range(2, portions):
-        block_start(which)
     settle_turned(g.gram_sum.at[0], g.basis_one)
     basis_one = g.basis_one[...]
 
@@ -428,20 +431,28 @@
         face = product(basis_one, jnp.concatenate(face, axis=1))
         for w in range(portions):
             flat_mixed[pl.ds(w * rank * SUBLANES + s, rank, stride=SUBLANES), :] = face[:, w * LANES : (w + 1) * LANES]
-    gram_second(1)
     pieces = rank // n
     lines = aligned(col * rows_two + chip * SUBLANES, SUBLANES)
     parts = pl.ds(core * portions, portions)
-    start_all(
-        [
-            remote(
-                g.mixed.at[:, pl.ds((row_peers[a] * n_col + col_peers[b]) * pieces, pieces)], g.joined.at[parts, :, lines, :],
-                ends(g.d_mixed), row_peers[a], col_peers[b],
-            )
-            for a, b in far
-        ]
-    )
+
+    def mixed_start(peers):
+        start_all(
+            [
+                remote(
+                    g.mixed.at[:, pl.ds((row_peers[a] * n_col + col_peers[b]) * pieces, pieces)],
+                    g.joined.at[parts, :, lines, :], ends(g.d_mixed), row_peers[a], col_peers[b],
+                )
+                for a, b in peers
+            ]
+        )
+
+    across = [at for at in far if at[1]]
+    fifth = len(across) // 5
+    mixed_start(across[:fifth])
+    gram_second(1)
+    mixed_start(across[fifth : 2 * fifth])
     gram_third(1)
+    mixed_start(across[2 * fifth :] + [at for at in far if not at[1]])
     g.joined[parts, :, lines, :] = g.mixed[:, pl.ds(me * pieces, pieces)]
     gram_end(1)
     settle_turned(g.gram_sum.at[1], g.basis_two)
@@ -452,15 +463,18 @@
     for end in range(2):
         wait_bytes(g.mixed.at[:, pl.ds(0, rank - pieces)], g.d_mixed.at[end])
     for a in range(pieces):
-        g.slab[a * rank : (a + 1) * rank, :] = product(
+        g.slab[a] = product(
             basis_two, jnp.concatenate([g.joined[w, a] for w in range(2 * portions)], axis=1)
         )
 
     bands, chunk = depth // BAND, rank // n_row
     own_chunk = aligned(row * chunk, chunk)
 
-    def band(ref, w):
-        return ref[:, w * BAND : (w + 1) * BAND]
+    def band(w):
+        return slice(w * BAND, (w + 1) * BAND)
+
+    def slab(w):
+        return g.slab[:, :, band(w)].reshape(pieces * rank, BAND)
 
     def added(terms):
         total = terms[0]
@@ -468,14 +482,19 @@
             total = total + term
         return total
 
-    def inner():
-        return added([right_product(band(g.iterate, w), band(g.iterate, w)) for w in range(bands)])
+    def scale(step):
+        for w in range(bands):
+            g.iterate[:, band(w)] = product(g.linv[...], g.image[step, w])
+        return added([right_product(g.iterate[:, band(w)], g.iterate[:, band(w)]) for w in range(bands)])
+
+    own_b = rank // n_col
+    own_pieces = pl.ds(col * pieces, pieces)
 
     def one(step, carry):
         turn = lax.rem(step, 2)
         cross = g.cross[...]
         for w in range(bands):
-            g.image_part[step, w] = product(cross, band(g.slab, w))
+            g.image_part[step, w] = product(cross, slab(w))
             start_all(
                 [
                     remote(
@@ -485,7 +504,7 @@
                     for d in range(1, n_row)
                 ]
             )
-        square = inner()
+        g.square[...] = scale(step)
         for w in range(bands):
             wait_bytes(g.image_parts.at[step, w, pl.ds(0, n_row - 1)], g.d_image_row.at[w, 1])
             g.image_planes[step, w, col] = added(
@@ -500,57 +519,65 @@
                     for d in range(1, n_col)
                 ]
             )
-        inverse = jnp.where(step == 0, unit(rank), inverse_factor(square))
-        g.linv[...] = inverse
+
+        @pl.when(step > 0)
+        def _():
+            g.linv[...] = inverse_factor(g.square[...])
+
         for w in range(bands):
             wait_bytes(g.image_planes.at[step, w, pl.ds(0, n_col - 1)], g.d_image_col.at[turn, w, 1])
-            g.image[step, w, own_chunk, :] = added([g.image_planes[step, w, q] for q in range(n_col)])
+            g.image[step + 1, w, own_chunk, :] = added([g.image_planes[step, w, q] for q in range(n_col)])
             start_all(
                 [
                     remote(
-                        g.image.at[step, w, own_chunk, :], g.image.at[step, w, own_chunk, :],
+                        g.image.at[step + 1, w, own_chunk, :], g.image.at[step + 1, w, own_chunk, :],
                         pair(g.d_image_all, w), row_peers[d], col,
                     )
                     for d in range(1, n_row)
                 ]
             )
+
+        @pl.when(step < bands)
+        def _():
+            lanes = aligned(step * BAND, BAND, LANES)
+            start_all(
+                [
+                    remote(
+                        g.slab.at[:, aligned(col_peers[d] * own_b, own_b), lanes], g.core_slab.at[own_pieces, :, lanes],
+                        ends(g.d_core), row, col_peers[d],
+                    )
+                    for d in range(1, n_col)
+                ]
+            )
+
         terms = []
         for w in range(bands):
-            wait_bytes(g.image.at[step, w, pl.ds(0, rank - chunk), :], g.d_image_all.at[w, 1])
-            now = product(g.linv[...], g.image[step, w])
-            g.iterate[:, w * BAND : (w + 1) * BAND] = now
-            terms.append(right_product(now, band(g.slab, w)))
-        g.cross[...] = added(terms)
+            wait_bytes(g.image.at[step + 1, w, pl.ds(0, rank - chunk), :], g.d_image_all.at[w, 1])
+            terms.append(right_product(g.image[step + 1, w], slab(w)))
+        g.cross[...] = product(g.linv[...], added(terms))
         for w in range(bands):
             wait_bytes(g.image_parts.at[step, w, pl.ds(0, n_row - 1)], g.d_image_row.at[w, 0])
             wait_bytes(g.image_planes.at[step, w, pl.ds(0, n_col - 1)], g.d_image_col.at[turn, w, 0])
-            wait_bytes(g.image.at[step, w, pl.ds(0, rank - chunk), :], g.d_image_all.at[w, 0])
+            wait_bytes(g.image.at[step + 1, w, pl.ds(0, rank - chunk), :], g.d_image_all.at[w, 0])
         return carry
 
-    g.iterate[...] = v_ref[...]
-    g.cross[...] = added([right_product(band(g.iterate, w), band(g.slab, w)) for w in range(bands)])
+    for w in range(bands):
+        g.image[0, w] = v_ref[:, band(w)]
+    g.linv[...] = unit(rank)
+    g.core_slab[own_pieces] = g.slab[:, aligned(col * own_b, own_b), :]
+    g.cross[...] = added([right_product(g.image[0, w], slab(w)) for w in range(bands)])
     lax.fori_loop(0, STEPS, one, 0)
-    g.core_own[...] = g.cross[...].T.reshape(pieces, rank, rank)
-    own_b = rank // n_col
-    own_pieces = pl.ds(col * pieces, pieces)
-    start_all(
-        [
-            remote(
-                g.core_own.at[:, aligned(col_peers[d] * own_b, own_b), :], g.core_all.at[own_pieces],
-                ends(g.d_core), row, col_peers[d],
-            )
-            for d in range(1, n_col)
-        ]
-    )
+    square = scale(STEPS)
     stores.append(pltpu.make_async_copy(g.iterate, outs[2], g.stored.at[2]))
     stores[-1].start()
-    g.core_all[own_pieces] = g.core_own[:, aligned(col * own_b, own_b), :]
-    g.linv[...] = inverse_factor(inner())
+    for end in (1, 0):
+        wait_bytes(g.core_slab.at[pl.ds(0, (n_col - 1) * pieces)], g.d_core.at[end])
+    whole = g.core_slab[...].reshape(n_col * pieces * own_b, depth)
+    g.core_all[...] = right_product(whole, g.iterate[...]).reshape(g.core_all.shape)
+    stores.append(pltpu.make_async_copy(g.core_all, outs[4], g.stored.at[4]))
+    stores[-1].start()
+    g.linv[...] = inverse_factor(square)
     stores.append(pltpu.make_async_copy(g.linv, outs[3], g.stored.at[3]))
-    stores[-1].start()
-    for end in (1, 0):
-        wait_bytes(g.core_all.at[pl.ds(0, (n_col - 1) * pieces)], g.d_core.at[end])
-    stores.append(pltpu.make_async_copy(g.core_all, outs[4], g.stored.at[4]))
     stores[-1].start()
     for copy in stores:
         copy.wait()
@@ -612,6 +639,7 @@
             and rows_two == plane * SUBLANES
             and rows_one % SUBLANES == 0
             and depth % BAND == 0
+            and depth // BAND <= STEPS
             and rank % (n_row * SUBLANES) == 0
             and rank % (n_col * SUBLANES) == 0
             and rank % n == 0

time: 116 us -> 112 us (0.966)
  Pallas kernels: 115 us -> 111 us
    pallas_call x1, Pallas kernels: 113 us -> 109 us  [shared(): pl.pallas_call(functools.partial(chain_kernel, n_row, n_col, tuple(scratc...]
where the time goes in v4:
time: 112 us; the launch traced here: 111 us
  Pallas kernels  111 us (99%)
    pallas_call x1, Pallas kernels, shared(): pl.pallas_call(functools.partial(chain_kernel, n_row, n_col, tuple(scratc...  109 us

profile of v4, /device:TPU:0, one launch (start us, length us, event | category | flops | bytes accessed | tf_op | source)
XLA Modules:
  0.0 111.4 jit_solution(496980253208579196)
XLA Ops:
  0.6 108.7 %chain.1 = (f32[64,128]{1,0:T(8,128)}, f32[64,128]{1,0:T(8,128)}, f32[64,768]{1,0:T(8,128)}, f32[64,64]{1,0:T(8,128)}, f32[8,16,64]{2,1,0:T(8,128)}) custom-call(f32[16,32,768]{2,1,0:T(8,128)} %refs_0_.1, f32[64,768]{1,0:T(8,128)} %bitcast.7, f32[16,64]{1,0:T(8,128)} %refs_2_.1, f32[32,64]{1,0:T(8,128)} %refs_3_.1), custom_call_target="tpu_custom_call" | custom-call | flops 1000000000 | bytes 10000000 | tf_op jit(solution)/shard_map/chain/pallas_call | solution.py:604
  109.4 2.1 %finish.1 = (f32[64,128]{1,0:T(8,128)}, f32[64,128]{1,0:T(8,128)}, f32[64,768]{1,0:T(8,128)}, f32[128,64]{1,0:T(8,128)}) custom-call(f32[64,128]{1,0:T(8,128)} %get-tuple-element.13.one_ref, f32[64,128]{1,0:T(8,128)} %get-tuple-element.14.two_ref, f32[64,768]{1,0:T(8,128)} %get-tuple-element.15.last_ref, f32[64,64]{1,0:T(8,128)} %get-tuple-element.16.linv_ref, ...), custom_call_target="tpu_custom_call" | custom-call | flops 10000000 | bytes 1000000 | tf_op jit(solution)/shard_map/finish/pallas_call | solution.py:616
